TPU v7x, 256 devices: a whole 4x4x8 slice. The times are simulated.
256 devices in a mesh: loader: 64 (over z, x, core), split: 4 (over y).
Axes of the slice: x: 4, y: 4, z: 8, core: 2. Of those that a mesh axis runs over, the one named last changes fastest.
Arguments:
- embeddings: bfloat16 [131072, 768], P(('loader', 'split')), may hold values from -6 to 6
- cluster_ids: int32 [131072, 1], P(('loader', 'split')), may hold values from 0 to 255; in each aligned block of 512 rows (0 to 511, 512 to 1023, ...) at most 4 rows name the same one
- ranks: int32 [131072], P(('loader', 'split')), may hold values from 0 to 131071, each once
Outputs:
- nearest: float32 [131072], P(('loader', 'split'))
Inputs may be any that keep to these rules, and one draw needn't show every extreme that they name: `cluster_ids`: among the 512 rows of one device no cluster appears more than 4 times. All ranks differ.
All inputs are finite; a program needn't handle non-finite values.
Results may differ from a plain program's by a relative error of at most 0.0014.
Values may be sent and summed in bfloat16 or wider, within the bound.
A program may use at most 64 MiB of HBM per device.

v0:
```python
import jax
import jax.numpy as jnp
from jax import lax
from jax.sharding import PartitionSpec as P

CLUSTERS = 256
CAP = 4


epsilon = 1e-06


def in_blocks(x, dim, size):
    dims = x.shape
    parts = x.reshape(*dims[:dim], size, dims[dim] // size, *dims[dim + 1 :])
    return jnp.moveaxis(parts, dim, 0)


def laid_out(parts, dim):
    dims = list(parts.shape[1:])
    dims[dim] *= parts.shape[0]
    return jnp.moveaxis(parts, 0, dim).reshape(dims)


def joined_exchange(x, axis, axes, splits, concats):
    sizes = [lax.axis_size(a) for a in axes]
    parts = in_blocks(x, splits[0], sizes[0])
    parts = jnp.moveaxis(in_blocks(parts, splits[1] + 1, sizes[1]), 0, 1)
    inside = parts.shape[2:]
    parts = parts.reshape(-1, *inside)
    parts = lax.all_to_all(parts, axis, split_axis=0, concat_axis=0, tiled=True)
    parts = laid_out(parts.reshape(*sizes, *inside), concats[0] + 1)
    return laid_out(parts, concats[1])


def tile_scores(queries, remote):
    return jnp.einsum("kqd,kmd->kqm", queries, remote, preferred_element_type=jnp.float32)


def row_maxima(scores, query_rank, member_rank):
    allowed = (member_rank[:, None, :] >= 0) & (member_rank[:, None, :] < query_rank[:, :, None])
    return jnp.max(jnp.where(allowed, scores, jnp.float32(-1.0)), axis=2)


def shards(embeddings, cluster_ids, ranks):
    loader_count = lax.axis_size("loader")
    split_count = lax.axis_size("split")
    rows_here = embeddings.shape[0]
    width = embeddings.shape[1]
    values = embeddings.astype(jnp.float32)
    unit = (values * lax.rsqrt(jnp.sum(values * values, axis=1, keepdims=True) + epsilon)).astype(
        jnp.bfloat16
    )
    cluster = cluster_ids[:, 0]
    row_index = jnp.arange(rows_here, dtype=jnp.int32)
    same_cluster = cluster[:, None] == cluster[None, :]
    earlier = row_index[None, :] < row_index[:, None]
    position = jnp.sum((same_cluster & earlier).astype(jnp.int32), axis=1)
    slot_count = CLUSTERS * CAP
    device_count = loader_count * split_count
    owner_flat = cluster % device_count
    cluster_slot = cluster // device_count
    owned = CLUSTERS // device_count
    target = (
        (cluster_slot * loader_count + owner_flat // split_count) * split_count
        + owner_flat % split_count
    ) * CAP + position
    send_rows = (
        jnp.zeros((slot_count, width), jnp.bfloat16)
        .at[target]
        .set(unit)
        .reshape(owned, loader_count, split_count, CAP, width)
    )
    send_rank = (
        jnp.full((slot_count,), -1, jnp.int32)
        .at[target]
        .set(ranks)
        .reshape(owned, loader_count, split_count, CAP)
    )
    arrived_rows, arrived_rank = (
        joined_exchange(send_rows, ("loader", "split"), ("loader", "split"), (1, 2), (1, 2)),
        joined_exchange(send_rank, ("loader", "split"), ("loader", "split"), (1, 2), (1, 2)),
    )
    members = arrived_rows.reshape(owned, -1, width)
    member_rank = arrived_rank.reshape(owned, -1)
    best = row_maxima(tile_scores(members, members), member_rank, member_rank)
    best = best.reshape(owned, loader_count, split_count, CAP)
    returned = joined_exchange(best, ("loader", "split"), ("loader", "split"), (1, 2), (1, 2))
    return returned.reshape(-1)[target]


def solution(mesh):
    return jax.shard_map(
        shards,
        mesh=mesh,
        in_specs=(
            P(("loader", "split"), None),
            P(("loader", "split"), None),
            P(("loader", "split")),
        ),
        out_specs=P(("loader", "split")),
        check_vma=False,
    )
```

profile of v0, /device:TPU:1, one launch (start us, length us, event | category | flops | bytes accessed | tf_op | source)
XLA Modules:
  0.0 108.8 jit_solution(2060933318394215782)
XLA Ops:
  0.0 0.0 copy-start
  0.0 1.0 convert_reduce_fusion
  1.0 0.7 compare_select_fusion
  1.7 2.6 %scatter_custom_fusion = s32[1024]{0:T(1024)S(1)} fusion(s32[512]{0:T(512)S(1)} %bitcast.39, s32[512]{0:T(512)} %param.5, s32[]{:T(128)} %constant.51.clone.1), kind=kCustom, calls=%fused_computation.29 | custom fusion | bytes 4608 | tf_op jit(solution)/shard_map/scatter | solution.py:77
  4.4 0.8 reshape_transpose_transpose_reshape_transpose_reshape_reshape.9
  5.1 15.6 %all-to-all-start = ((s32[256,1,1,1,4]{4,3,2,1,0:T(1,128)}), s32[256,1,1,1,4]{4,3,2,1,0:T(1,128)S(1)}, u32[]{:S(2)}, u32[]{:S(2)}) async-start(s32[256,1,1,1,4]{4,3,2,1,0:T(1,128)} %bitcast.3), calls=%async_computation | async-start | bytes 262144 | tf_op jit(solution)/shard_map/all_to_all | solution.py:31
  20.8 1.4 %fusion = f32[512]{0:T(512)S(1)} fusion(bf16[512,768]{1,0:T(8,128)(2,1)} %param.3), kind=kLoop, calls=%fused_computation.6 | loop fusion | flops 1179136 | bytes 788480 | tf_op jit(solution)/shard_map/reduce_sum | solution.py:51
  22.2 0.0 copy-done
  22.2 3.1 %scatter_custom_fusion.1 = bf16[1024,768]{1,0:T(8,128)(2,1)S(1)} fusion(s32[512]{0:T(512)S(1)} %bitcast.40, bf16[512,768]{1,0:T(8,128)(2,1)S(1)} %copy-done, f32[512]{0:T(512)S(1)} %add_rsqrt_fusion, bf16[]{:T(256)} %constant.62.clone.1), kind=kCustom, calls=%fused_computation.11 | custom fusion | flops 1179648 | bytes 2361346 | tf_op jit(solution)/shard_map/scatter | solution.py:71
  25.3 1.4 %reshape_transpose_transpose_reshape_transpose_reshape_reshape.10 = bf16[256,1,1,1,4,768]{5,4,0,3,2,1:T(4,128)(2,1)} reshape(bf16[1024,768]{1,0:T(8,128)(2,1)S(1)} %scatter_custom_fusion.1) | data formatting | bytes 3145728 | tf_op jit(solution)/shard_map/reshape;transpose;transpose;reshape;transpose;reshape;reshape | solution.py:30
  26.6 6.9 %all-to-all-done = s32[256,1,1,1,4]{4,3,2,1,0:T(1,128)S(1)} async-done(((s32[256,1,1,1,4]{4,3,2,1,0:T(1,128)}), s32[256,1,1,1,4]{4,3,2,1,0:T(1,128)S(1)}, u32[]{:S(2)}, u32[]{:S(2)}) %all-to-all-start) | async-done | bytes 4128 | tf_op jit(solution)/shard_map/all_to_all | solution.py:31
  33.5 6.8 %all-to-all-start.1 = ((bf16[256,1,1,1,4,768]{5,4,3,2,1,0:T(4,128)(2,1)}), bf16[256,1,1,1,4,768]{5,4,3,2,1,0:T(4,128)(2,1)S(1)}, u32[]{:S(2)}, u32[]{:S(2)}) async-start(bf16[256,1,1,1,4,768]{5,4,3,2,1,0:T(4,128)(2,1)} %bitcast.8), calls=%async_computation.1 | async-start | bytes 3145728 | tf_op jit(solution)/shard_map/all_to_all | solution.py:31
  40.4 0.2 broadcast_in_dim_reshape_reshape.2
  40.5 41.9 %all-to-all-done.1 = bf16[256,1,1,1,4,768]{5,4,3,2,1,0:T(4,128)(2,1)S(1)} async-done(((bf16[256,1,1,1,4,768]{5,4,3,2,1,0:T(4,128)(2,1)}), bf16[256,1,1,1,4,768]{5,4,3,2,1,0:T(4,128)(2,1)S(1)}, u32[]{:S(2)}, u32[]{:S(2)}) %all-to-all-start.1) | async-done | bytes 1572896 | tf_op jit(solution)/shard_map/all_to_all | solution.py:31
  82.4 0.4 reshape.57
  82.8 2.3 %select_reduce_fusion = f32[1024]{0:T(1024)S(1)} fusion(s32[1024]{0:T(1024)S(1)} %broadcast_in_dim_reshape_reshape.2, pred[1024]{0:T(1024)(128)(4,1)S(1)} %broadcast_compare_fusion, bf16[1024,768]{1,0:T(8,128)(2,1)S(1)} %reshape.57), kind=kOutput, calls=%fused_computation.3 | convolution fusion | flops 1614806016 | bytes 1582080 | tf_op jit(solution)/shard_map/kqd,kmd->kqm/dot_general | solution.py:37
  85.0 0.8 reshape_transpose_transpose_reshape_transpose_reshape_reshape.11
  85.8 6.7 %all-to-all-start.2 = ((f32[256,1,1,1,4]{4,3,2,1,0:T(1,128)}), f32[256,1,1,1,4]{4,3,2,1,0:T(1,128)S(1)}, u32[]{:S(2)}, u32[]{:S(2)}) async-start(f32[256,1,1,1,4]{4,3,2,1,0:T(1,128)} %bitcast.13), calls=%async_computation.2 | async-start | bytes 262144 | tf_op jit(solution)/shard_map/all_to_all | solution.py:31
  92.5 12.7 %all-to-all-done.2 = f32[256,1,1,1,4]{4,3,2,1,0:T(1,128)S(1)} async-done(((f32[256,1,1,1,4]{4,3,2,1,0:T(1,128)}), f32[256,1,1,1,4]{4,3,2,1,0:T(1,128)S(1)}, u32[]{:S(2)}, u32[]{:S(2)}) %all-to-all-start.2) | async-done | bytes 4128 | tf_op jit(solution)/shard_map/all_to_all | solution.py:31
  105.2 0.2 reshape_reshape.4
  105.4 3.4 %gather_fusion = f32[512]{0:T(512)} fusion(f32[1024]{0:T(1024)S(1)} %reshape_reshape.4, s32[1024]{0:T(1024)S(1)} %pad_clamp_fusion), kind=kCustom, calls=%fused_computation | custom fusion | bytes 6144 | tf_op jit(solution)/shard_map/gather | solution.py:89
  (3 shorter events, 0.0 us)
Async XLA Ops:
  0.0 22.2 %copy-start = (bf16[512,768]{1,0:T(8,128)(2,1)S(1)}, bf16[512,768]{1,0:T(8,128)(2,1)}, u32[]{:S(2)}) copy-start(bf16[512,768]{1,0:T(8,128)(2,1)} %param.3) | copy-start | bytes 2359300
  5.1 28.4 %all-to-all-start = ((s32[256,1,1,1,4]{4,3,2,1,0:T(1,128)}), s32[256,1,1,1,4]{4,3,2,1,0:T(1,128)S(1)}, u32[]{:S(2)}, u32[]{:S(2)}) async-start(s32[256,1,1,1,4]{4,3,2,1,0:T(1,128)} %bitcast.3), calls=%async_computation | async-start | bytes 262144 | tf_op jit(solution)/shard_map/all_to_all | solution.py:31
  33.5 48.9 %all-to-all-start.1 = ((bf16[256,1,1,1,4,768]{5,4,3,2,1,0:T(4,128)(2,1)}), bf16[256,1,1,1,4,768]{5,4,3,2,1,0:T(4,128)(2,1)S(1)}, u32[]{:S(2)}, u32[]{:S(2)}) async-start(bf16[256,1,1,1,4,768]{5,4,3,2,1,0:T(4,128)(2,1)} %bitcast.8), calls=%async_computation.1 | async-start | bytes 3145728 | tf_op jit(solution)/shard_map/all_to_all | solution.py:31
  85.8 19.4 %all-to-all-start.2 = ((f32[256,1,1,1,4]{4,3,2,1,0:T(1,128)}), f32[256,1,1,1,4]{4,3,2,1,0:T(1,128)S(1)}, u32[]{:S(2)}, u32[]{:S(2)}) async-start(f32[256,1,1,1,4]{4,3,2,1,0:T(1,128)} %bitcast.13), calls=%async_computation.2 | async-start | bytes 262144 | tf_op jit(solution)/shard_map/all_to_all | solution.py:31
where the time goes:
time: 109 us
  waiting for transfers between devices  61.5 us (56%)
  starting transfers between devices  29.1 us (27%)
  local copies, waits for them, and re-layouts  9.62 us (9%)
  other arithmetic  6.23 us (6%)
  matrix products  2.27 us (2%)
    all_to_all x3, waiting for transfers between devices, joined_exchange(): parts = lax.all_to_all(parts, axis, split_axis=0, concat_axis=0, tiled=True)  61.5 us
    all_to_all x3, starting transfers between devices, joined_exchange(): parts = lax.all_to_all(parts, axis, split_axis=0, concat_axis=0, tiled=True)  29.1 us
    gather x1, local copies, waits for them, and re-layouts, shards(): return returned.reshape(-1)[target]  3.42 us
    scatter x1, other arithmetic, shards(): send_rows = jnp.zeros((slot_count, width), jnp.bfloat16).at[target].set(u...  3.1 us
    another operation x3, local copies, waits for them, and re-layouts, joined_exchange(): parts = parts.reshape(-1, *inside)  2.91 us
    scatter x1, local copies, waits for them, and re-layouts, shards(): send_rank = jnp.full((slot_count,), -1, jnp.int32).at[target].set(ranks)....  2.6 us
    dot_general x1, matrix products, tile_scores(): jnp.einsum('kqd,kmd->kqm', queries, remote, preferred_element_type=jnp.fl...  2.27 us
  transfers between devices with their start and end apart: 3, of which 3 were waited for; matrix products, arithmetic and copies ran while one was open for 6% of the time, Pallas kernels for 0%

commit v1 on v0

v1 whole, which is shorter than its diff:
```python
import functools

import jax
import jax.numpy as jnp
from jax import lax
from jax.experimental import pallas as pl
from jax.experimental.pallas import tpu as pltpu
from jax.sharding import PartitionSpec as P

MESH = pl.DeviceIdType.MESH
CLUSTERS = 256
CAP = 4
WIDTH = 768
ROWS_DEV = 512
PLANES = 8
PEERS = 32
SLOTS = PEERS * CAP
BLOCKS = ROWS_DEV // 128
ROOM = 128
EMPTY = float(1 << 17)
GROUPS = ((0,), (1, 7), (2, 6), (3, 5), (4,))
epsilon = 1e-06


def place():
    row = lax.axis_index("loader")
    y = lax.axis_index("split")
    return lax.div(row, 8), y, lax.rem(lax.div(row, 2), 4), lax.rem(row, 2)


def device(z, y, x, c):
    return ((z * 4 + x) * 2 + c, y)


def across(here, s):
    z, y, x, c = here
    return device(lax.rem(z + s, PLANES), y, x, c)


def within(here, j, sign):
    z, y, x, c = here
    dy, dx, dc = lax.rem(j, 4), lax.rem(lax.div(j, 4), 4), lax.div(j, 16)
    return device(
        z,
        lax.rem(y + 4 + sign * dy, 4),
        lax.rem(x + 4 + sign * dx, 4),
        lax.rem(c + dc, 2),
    )


def send(src, dst, sent, landed, to):
    return pltpu.make_async_remote_copy(
        src_ref=src,
        dst_ref=dst,
        send_sem=sent,
        recv_sem=landed,
        device_id=to,
        device_id_type=MESH,
    )


def product(a, b):
    return lax.dot_general(
        a, b, (((1,), (1,)), ((), ())), preferred_element_type=jnp.float32
    )


def iota(shape, dim):
    return lax.broadcasted_iota(jnp.int32, shape, dim)


def own_lanes(tiles_ref):
    group = iota((PLANES, SLOTS), 1) // CAP
    total = jnp.zeros((PLANES, SLOTS), jnp.float32)
    for j in range(PEERS):
        total = jnp.where(group == j, tiles_ref[j], total)
    return total


def kernel(
    emb_hbm, cid_ref, rank_ref, out_ref, flag_ref,
    raw, unit, meta_out, meta_in, rows_out, rows_in, dense, arrived, members,
    ranks_out, ranks_in, best_out, best_in, back_out, back_in,
    raw_sem, meta_sent, meta_landed, rows_sent, rows_landed, dense_sent, dense_landed,
    ranks_sent, ranks_landed, best_sent, best_landed, back_sent, back_landed,
):
    here = place()
    z, y, x, c = here
    loads = [
        pltpu.make_async_copy(
            emb_hbm.at[pl.ds(b * 128, 128)], raw.at[pl.ds(b * 128, 128)], raw_sem.at[b]
        )
        for b in range(BLOCKS)
    ]
    for load in loads:
        load.start()
    barrier = pltpu.get_barrier_semaphore()

    def greet_across(s, carry):
        pl.semaphore_signal(barrier, inc=1, device_id=across(here, s), device_id_type=MESH)
        return carry

    def greet_within(j, carry):
        pl.semaphore_signal(barrier, inc=1, device_id=within(here, j, 1), device_id_type=MESH)
        return carry

    lax.fori_loop(1, PLANES, greet_across, 0)
    lax.fori_loop(1, PEERS, greet_within, 0)

    cid = cid_ref[...]
    owner = cid & (PEERS - 1)
    step = ((cid >> 5) - z) & (PLANES - 1)
    peer = (
        (((owner >> 4) - c) & 1) * 16 + (((owner >> 2) - x) & 3) * 4 + ((owner - y) & 3)
    )
    turned = jnp.concatenate([cid, step], axis=0).T
    before = iota((128, 128), 0) < iota((128, 128), 1)
    slot_rows, pack_rows, over = [], [], jnp.zeros((1, 128), jnp.float32)
    for b in range(BLOCKS):
        same = jnp.zeros((128, 128), jnp.float32)
        along = jnp.zeros((128, 128), jnp.float32)
        for a in range(b + 1):
            alike = turned[:, a : a + 1] == cid[b : b + 1]
            aside = turned[:, BLOCKS + a : BLOCKS + a + 1] == step[b : b + 1]
            if a == b:
                alike, aside = alike & before, aside & before
            same += jnp.where(alike, 1.0, 0.0)
            along += jnp.where(aside, 1.0, 0.0)
        position = jnp.sum(same, axis=0, keepdims=True).astype(jnp.int32)
        count = jnp.sum(along, axis=0, keepdims=True).astype(jnp.int32)
        steps = step[b : b + 1] * SLOTS
        slot_rows.append(steps + peer[b : b + 1] * CAP + position)
        pack_rows.append(jnp.where(count < ROOM, steps + count, -1))
        over = jnp.maximum(over, jnp.where(count < ROOM, 0.0, 2 * EMPTY))
    over = jnp.max(over, axis=1, keepdims=True)
    slot_turned = jnp.concatenate(slot_rows + pack_rows, axis=0).T
    rank_turned = (rank_ref[...].astype(jnp.float32) - EMPTY).T
    lane = iota((128, 128), 1)
    for s in range(PLANES):
        name = jnp.zeros((128, 128), jnp.float32)
        rank = jnp.zeros((128, 128), jnp.float32)
        for b in range(BLOCKS):
            slots = slot_turned[:, b : b + 1]
            packs = slot_turned[:, BLOCKS + b : BLOCKS + b + 1]
            name = jnp.where(packs == s * SLOTS + lane, (slots - (s * SLOTS - 1)).astype(jnp.float32), name)
            rank = jnp.where(slots == s * SLOTS + lane, rank_turned[:, b : b + 1], rank)
        ref = meta_in if s == 0 else meta_out
        ref[s, 0:1] = jnp.sum(name, axis=0, keepdims=True) - 1.0
        ref[s, 1:2] = jnp.sum(rank, axis=0, keepdims=True) + (EMPTY + over)
    for b in range(BLOCKS):
        loads[b].wait()
        values = raw[b * 128 : (b + 1) * 128].astype(jnp.float32)
        scale = lax.rsqrt(jnp.sum(values * values, axis=1, keepdims=True) + epsilon)
        unit[b * 128 : (b + 1) * 128] = (values * scale).astype(jnp.bfloat16)

    pl.semaphore_wait(barrier, PLANES - 1 + PEERS - 1)
    metas, rows = {}, {}
    order = [s for group in GROUPS for s in group if s]
    for s in order:
        metas[s] = send(meta_out.at[s], meta_in.at[s], meta_sent.at[s], meta_landed.at[s], across(here, s))
        metas[s].start()
    pack = jnp.concatenate(pack_rows, axis=1)
    for group in GROUPS[1:] + GROUPS[:1]:
        chosen = jnp.concatenate(
            [jnp.where(pack == s * SLOTS + iota((ROOM, ROWS_DEV), 0), 1.0, 0.0) for s in group], axis=0
        ).astype(jnp.bfloat16)
        packed = jnp.dot(chosen, unit[...], preferred_element_type=jnp.float32).astype(jnp.bfloat16)
        for n, s in enumerate(group):
            ref = rows_in if s == 0 else rows_out
            ref[s] = packed[n * ROOM : (n + 1) * ROOM]
            if s:
                rows[s] = send(rows_out.at[s], rows_in.at[s], rows_sent.at[s], rows_landed.at[s], across(here, s))
                rows[s].start()

    def spread(s):
        chosen = jnp.where(
            meta_in[s, 0:1, :ROOM] == iota((SLOTS, ROOM), 0).astype(jnp.float32), 1.0, 0.0
        ).astype(jnp.bfloat16)
        placed = jnp.dot(chosen, rows_in[s], preferred_element_type=jnp.float32).astype(jnp.bfloat16)
        dense[s] = placed.reshape(PEERS, CAP, WIDTH)
        arrived[s, 0] = placed[:CAP]

        def deliver(j, carry):
            send(dense.at[s, j], arrived.at[s, j], dense_sent.at[s], dense_landed.at[s], within(here, j, 1)).start()
            return carry

        lax.fori_loop(1, PEERS, deliver, 0)

    for s in order:
        metas[s].wait_recv()
    for s in range(PLANES):
        ranks_out[s : s + 1] = meta_in[s, 1:2]
    ranks_in[0] = ranks_out[...]

    def deliver_ranks(j, carry):
        send(ranks_out, ranks_in.at[j], ranks_sent, ranks_landed, within(here, j, 1)).start()
        return carry

    lax.fori_loop(1, PEERS, deliver_ranks, 0)
    others = pl.ds(1, PEERS - 1)
    spread(0)

    best = [jnp.full((1, SLOTS), -1.0, jnp.float32)] * PLANES
    seen = []
    rank_row = rank_col = None
    for turn in range(1, len(GROUPS) + 1):
        if turn < len(GROUPS):
            for s in GROUPS[turn]:
                rows[s].wait_recv()
                spread(s)
        if turn == 1:
            send(ranks_in.at[others], ranks_in.at[others], ranks_sent, ranks_landed, within(here, 1, 1)).wait_recv()
            rank_row = own_lanes(ranks_in)
            rank_col = rank_row.T
            highest = jnp.full((PLANES, SLOTS), 0.0, jnp.float32)
            for j in range(PEERS):
                highest = jnp.maximum(highest, ranks_in[j])
            flag_ref[...] = jnp.where(highest >= 2 * EMPTY, 1.0, 0.0)
        group = GROUPS[turn - 1]
        known = len(seen)
        for s in group:
            send(dense.at[s, others], arrived.at[s, others], dense_sent.at[s], dense_landed.at[s], within(here, 1, 1)).wait_recv()
            members[len(seen) * SLOTS : (len(seen) + 1) * SLOTS] = arrived[s].reshape(SLOTS, WIDTH)
            seen.append(s)
        new = members[known * SLOTS : len(seen) * SLOTS]
        scores = product(members[: len(seen) * SLOTS], new)
        for n, q in enumerate(group):
            top = jnp.full((SLOTS, SLOTS), -1.0, jnp.float32)
            for k, m in enumerate(seen):
                part = scores[k * SLOTS : (k + 1) * SLOTS, n * SLOTS : (n + 1) * SLOTS]
                earlier = rank_col[:, m : m + 1] < rank_row[q : q + 1]
                top = jnp.maximum(top, jnp.where(earlier, part, -1.0))
            best[q] = jnp.maximum(best[q], jnp.max(top, axis=0, keepdims=True))
        if known:
            scores = product(new, members[: known * SLOTS])
            for k, q in enumerate(seen[:known]):
                top = jnp.full((SLOTS, SLOTS), -1.0, jnp.float32)
                for n, m in enumerate(group):
                    part = scores[n * SLOTS : (n + 1) * SLOTS, k * SLOTS : (k + 1) * SLOTS]
                    earlier = rank_col[:, m : m + 1] < rank_row[q : q + 1]
                    top = jnp.maximum(top, jnp.where(earlier, part, -1.0))
                best[q] = jnp.maximum(best[q], jnp.max(top, axis=0, keepdims=True))

    best_out[...] = jnp.concatenate(best, axis=0)

    def answer(j, carry):
        send(best_out, best_in.at[j], best_sent, best_landed, within(here, j, -1)).start()
        return carry

    lax.fori_loop(1, PEERS, answer, 0)
    best_in[0] = best_out[...]
    for s in order:
        metas[s].wait_send()
        rows[s].wait_send()
    for s in range(PLANES):
        send(dense.at[s, others], arrived.at[s, others], dense_sent.at[s], dense_landed.at[s], within(here, 1, 1)).wait_send()
    send(ranks_in.at[others], ranks_in.at[others], ranks_sent, ranks_landed, within(here, 1, 1)).wait_send()
    whole = send(best_in.at[others], best_in.at[others], best_sent, best_landed, within(here, 1, 1))
    whole.wait_recv()
    results = own_lanes(best_in)
    backs = []
    for s in range(PLANES):
        ref = back_in if s == 0 else back_out
        ref[s] = results[s : s + 1]
        if s:
            back = send(back_out.at[s], back_in.at[s], back_sent.at[s], back_landed.at[s], across(here, PLANES - s))
            back.start()
            backs.append(back)
    whole.wait_send()
    for back in backs:
        back.wait()
    result_col = jnp.concatenate([back_in[s] for s in range(PLANES)], axis=0).T
    slot = iota((SLOTS, 128), 0)
    for b in range(BLOCKS):
        found = jnp.zeros((SLOTS, 128), jnp.float32)
        for s in range(PLANES):
            found = jnp.where(slot_rows[b] == s * SLOTS + slot, result_col[:, s : s + 1], found)
        out_ref[b : b + 1] = jnp.sum(found, axis=0, keepdims=True)


def shards(embeddings, cluster_ids, ranks):
    dma = pltpu.SemaphoreType.DMA
    best, flag = pl.pallas_call(
        kernel,
        out_shape=(
            jax.ShapeDtypeStruct((BLOCKS, 128), jnp.float32),
            jax.ShapeDtypeStruct((PLANES, SLOTS), jnp.float32),
        ),
        in_specs=[
            pl.BlockSpec(memory_space=pl.ANY),
            pl.BlockSpec(memory_space=pltpu.VMEM),
            pl.BlockSpec(memory_space=pltpu.VMEM),
        ],
        out_specs=(pl.BlockSpec(memory_space=pltpu.VMEM),) * 2,
        scratch_shapes=[
            pltpu.VMEM((ROWS_DEV, WIDTH), jnp.bfloat16),
            pltpu.VMEM((ROWS_DEV, WIDTH), jnp.bfloat16),
            pltpu.VMEM((PLANES, 2, SLOTS), jnp.float32),
            pltpu.VMEM((PLANES, 2, SLOTS), jnp.float32),
            pltpu.VMEM((PLANES, ROOM, WIDTH), jnp.bfloat16),
            pltpu.VMEM((PLANES, ROOM, WIDTH), jnp.bfloat16),
            pltpu.VMEM((PLANES, PEERS, CAP, WIDTH), jnp.bfloat16),
            pltpu.VMEM((PLANES, PEERS, CAP, WIDTH), jnp.bfloat16),
            pltpu.VMEM((PLANES * SLOTS, WIDTH), jnp.bfloat16),
            pltpu.VMEM((PLANES, SLOTS), jnp.float32),
            pltpu.VMEM((PEERS, PLANES, SLOTS), jnp.float32),
            pltpu.VMEM((PLANES, SLOTS), jnp.float32),
            pltpu.VMEM((PEERS, PLANES, SLOTS), jnp.float32),
            pltpu.VMEM((PLANES, 1, SLOTS), jnp.float32),
            pltpu.VMEM((PLANES, 1, SLOTS), jnp.float32),
            dma((BLOCKS,)),
            dma((PLANES,)), dma((PLANES,)),
            dma((PLANES,)), dma((PLANES,)),
            dma((PLANES,)), dma((PLANES,)),
            dma, dma,
            dma, dma,
            dma((PLANES,)), dma((PLANES,)),
        ],
        compiler_params=pltpu.CompilerParams(
            collective_id=0, has_side_effects=True, vmem_limit_bytes=67043328
        ),
    )(embeddings, cluster_ids.reshape(BLOCKS, 128), ranks.reshape(BLOCKS, 128))
    return best.reshape(ROWS_DEV)


def solution(mesh):
    return jax.shard_map(
        shards,
        mesh=mesh,
        in_specs=(
            P(("loader", "split"), None),
            P(("loader", "split"), None),
            P(("loader", "split")),
        ),
        out_specs=P(("loader", "split")),
        check_vma=False,
    )
```

time: 109 us -> 70.3 us (0.64)
  Pallas kernels: 0 us -> 68.9 us
  waiting for transfers between devices: 61.5 us -> 0 us
  starting transfers between devices: 29.1 us -> 0 us
  local copies, waits for them, and re-layouts: 9.62 us -> 1.24 us
  other arithmetic: 6.23 us -> 0 us
  matrix products: 2.27 us -> 0 us
    pallas_call x0 -> x1, Pallas kernels: none -> 68.9 us  [shards(): pl.pallas_call(kernel, out_shape=(jax.ShapeDtypeStruct((BLOCKS, 128), jnp...]
    all_to_all x3 -> x0, waiting for transfers between devices: 61.5 us -> none  [joined_exchange(): parts = lax.all_to_all(parts, axis, split_axis=0, concat_axis=0, tiled=True)]
    all_to_all x3 -> x0, starting transfers between devices: 29.1 us -> none  [joined_exchange(): parts = lax.all_to_all(parts, axis, split_axis=0, concat_axis=0, tiled=True)]
    another operation x6 -> x0, local copies, waits for them, and re-layouts: 3.59 us -> none  [the longest x3 2.91 us: joined_exchange(): parts = parts.reshape(-1, *inside)]
    gather x1 -> x0, local copies, waits for them, and re-layouts: 3.42 us -> none  [shards(): return returned.reshape(-1)[target]]
    scatter x1 -> x0, other arithmetic: 3.1 us -> none  [shards(): send_rows = jnp.zeros((slot_count, width), jnp.bfloat16).at[target].set(u...]
    scatter x1 -> x0, local copies, waits for them, and re-layouts: 2.6 us -> none  [shards(): send_rank = jnp.full((slot_count,), -1, jnp.int32).at[target].set(ranks)....]
    reduce_sum x2 -> x0, other arithmetic: 2.38 us -> none  [the longest x1 1.36 us: shards(): jnp.sum(values * values, axis=1, keepdims=True) + epsilon]
  transfers between devices with their start and end apart: 3 -> 0, of which waited for: 3 -> 0; matrix products, arithmetic and copies ran while one was open for 6% -> 0% of each run, Pallas kernels for 0% -> 0%
where the time goes in v1:
time: 70.3 us; the launch traced here: 70.1 us
  Pallas kernels  68.9 us (98%)
  local copies, waits for them, and re-layouts  1.24 us (2%)
    pallas_call x1, Pallas kernels, shards(): pl.pallas_call(kernel, out_shape=(jax.ShapeDtypeStruct((BLOCKS, 128), jnp...  68.9 us

profile of v1, /device:TPU:1, one launch (start us, length us, event | category | flops | bytes accessed | tf_op | source)
XLA Modules:
  0.0 70.1 jit_solution(14758418164898048881)
XLA Ops:
  0.0 68.9 %shard_map.37 = (f32[4,128]{1,0:T(4,128)}, f32[8,128]{1,0:T(8,128)}) custom-call(bf16[512,768]{1,0:T(8,128)(2,1)} %emb_hbm.1, s32[4,128]{1,0:T(4,128)} %bitcast.3, s32[4,128]{1,0:T(4,128)} %bitcast.4), custom_call_target="tpu_custom_call" | custom-call | tf_op jit(solution)/shard_map/pallas_call | solution.py:283
  68.9 0.0 copy-start
  68.9 0.7 copy-done
  69.6 0.6 copy.5
Async XLA Ops:
  68.9 0.7 copy-start

commit v2 on v1

--- a/solution.py
+++ b/solution.py
@@ -16,7 +16,7 @@
 PEERS = 32
 SLOTS = PEERS * CAP
 BLOCKS = ROWS_DEV // 128
-ROOM = 128
+ROOM = 80
 EMPTY = float(1 << 17)
 GROUPS = ((0,), (1, 7), (2, 6), (3, 5), (4,))
 epsilon = 1e-06
@@ -78,7 +78,7 @@
 
 
 def kernel(
-    emb_hbm, cid_ref, rank_ref, out_ref, flag_ref,
+    room, emb_hbm, cid_ref, rank_ref, out_ref, flag_ref,
     raw, unit, meta_out, meta_in, rows_out, rows_in, dense, arrived, members,
     ranks_out, ranks_in, best_out, best_in, back_out, back_in,
     raw_sem, meta_sent, meta_landed, rows_sent, rows_landed, dense_sent, dense_landed,
@@ -130,8 +130,8 @@
         count = jnp.sum(along, axis=0, keepdims=True).astype(jnp.int32)
         steps = step[b : b + 1] * SLOTS
         slot_rows.append(steps + peer[b : b + 1] * CAP + position)
-        pack_rows.append(jnp.where(count < ROOM, steps + count, -1))
-        over = jnp.maximum(over, jnp.where(count < ROOM, 0.0, 2 * EMPTY))
+        pack_rows.append(jnp.where(count < room, steps + count, -1))
+        over = jnp.maximum(over, jnp.where(count < room, 0.0, 2 * EMPTY))
     over = jnp.max(over, axis=1, keepdims=True)
     slot_turned = jnp.concatenate(slot_rows + pack_rows, axis=0).T
     rank_turned = (rank_ref[...].astype(jnp.float32) - EMPTY).T
@@ -162,19 +162,19 @@
     pack = jnp.concatenate(pack_rows, axis=1)
     for group in GROUPS[1:] + GROUPS[:1]:
         chosen = jnp.concatenate(
-            [jnp.where(pack == s * SLOTS + iota((ROOM, ROWS_DEV), 0), 1.0, 0.0) for s in group], axis=0
+            [jnp.where(pack == s * SLOTS + iota((room, ROWS_DEV), 0), 1.0, 0.0) for s in group], axis=0
         ).astype(jnp.bfloat16)
         packed = jnp.dot(chosen, unit[...], preferred_element_type=jnp.float32).astype(jnp.bfloat16)
         for n, s in enumerate(group):
             ref = rows_in if s == 0 else rows_out
-            ref[s] = packed[n * ROOM : (n + 1) * ROOM]
+            ref[s] = packed[n * room : (n + 1) * room]
             if s:
                 rows[s] = send(rows_out.at[s], rows_in.at[s], rows_sent.at[s], rows_landed.at[s], across(here, s))
                 rows[s].start()
 
     def spread(s):
         chosen = jnp.where(
-            meta_in[s, 0:1, :ROOM] == iota((SLOTS, ROOM), 0).astype(jnp.float32), 1.0, 0.0
+            meta_in[s, 0:1, :room] == iota((SLOTS, room), 0).astype(jnp.float32), 1.0, 0.0
         ).astype(jnp.bfloat16)
         placed = jnp.dot(chosen, rows_in[s], preferred_element_type=jnp.float32).astype(jnp.bfloat16)
         dense[s] = placed.reshape(PEERS, CAP, WIDTH)
@@ -215,7 +215,7 @@
             highest = jnp.full((PLANES, SLOTS), 0.0, jnp.float32)
             for j in range(PEERS):
                 highest = jnp.maximum(highest, ranks_in[j])
-            flag_ref[...] = jnp.where(highest >= 2 * EMPTY, 1.0, 0.0)
+            flag_ref[...] = jnp.full((PLANES, SLOTS), jnp.max(jnp.where(highest >= 2 * EMPTY, 1.0, 0.0)))
         group = GROUPS[turn - 1]
         known = len(seen)
         for s in group:
@@ -278,10 +278,10 @@
         out_ref[b : b + 1] = jnp.sum(found, axis=0, keepdims=True)
 
 
-def shards(embeddings, cluster_ids, ranks):
+def exchange(room, number, embeddings, cluster_ids, ranks):
     dma = pltpu.SemaphoreType.DMA
-    best, flag = pl.pallas_call(
-        kernel,
+    return pl.pallas_call(
+        functools.partial(kernel, room),
         out_shape=(
             jax.ShapeDtypeStruct((BLOCKS, 128), jnp.float32),
             jax.ShapeDtypeStruct((PLANES, SLOTS), jnp.float32),
@@ -297,8 +297,8 @@
             pltpu.VMEM((ROWS_DEV, WIDTH), jnp.bfloat16),
             pltpu.VMEM((PLANES, 2, SLOTS), jnp.float32),
             pltpu.VMEM((PLANES, 2, SLOTS), jnp.float32),
-            pltpu.VMEM((PLANES, ROOM, WIDTH), jnp.bfloat16),
-            pltpu.VMEM((PLANES, ROOM, WIDTH), jnp.bfloat16),
+            pltpu.VMEM((PLANES, room, WIDTH), jnp.bfloat16),
+            pltpu.VMEM((PLANES, room, WIDTH), jnp.bfloat16),
             pltpu.VMEM((PLANES, PEERS, CAP, WIDTH), jnp.bfloat16),
             pltpu.VMEM((PLANES, PEERS, CAP, WIDTH), jnp.bfloat16),
             pltpu.VMEM((PLANES * SLOTS, WIDTH), jnp.bfloat16),
@@ -317,10 +317,16 @@
             dma((PLANES,)), dma((PLANES,)),
         ],
         compiler_params=pltpu.CompilerParams(
-            collective_id=0, has_side_effects=True, vmem_limit_bytes=67043328
+            collective_id=number, has_side_effects=True, vmem_limit_bytes=67043328
         ),
-    )(embeddings, cluster_ids.reshape(BLOCKS, 128), ranks.reshape(BLOCKS, 128))
-    return best.reshape(ROWS_DEV)
+    )(embeddings, cluster_ids, ranks)
+
+
+def shards(embeddings, cluster_ids, ranks):
+    given = embeddings, cluster_ids.reshape(BLOCKS, 128), ranks.reshape(BLOCKS, 128)
+    nearest, over = exchange(ROOM, 0, *given)
+    nearest = lax.cond(over[0, 0] > 0, lambda best: exchange(SLOTS, 1, *given)[0], lambda best: best, nearest)
+    return nearest.reshape(ROWS_DEV)
 
 
 def solution(mesh):

time: 70.3 us -> 59 us (0.84)
  Pallas kernels: 68.9 us -> 56.1 us
    pallas_call x1, Pallas kernels: 68.9 us -> 56.1 us  [exchange(): pl.pallas_call(functools.partial(kernel, room), out_shape=(jax.ShapeDtype...]
    slice x0 -> x1, local copies, waits for them, and re-layouts: none -> 1.2 us  [shards(): over[0, 0] > 0]
where the time goes in v2:
time: 59 us; the launch traced here: 58.8 us
  Pallas kernels  56.1 us (95%)
  local copies, waits for them, and re-layouts  1.8 us (3%)
  between operations  0.67 us (1%)
    pallas_call x1, Pallas kernels, exchange(): pl.pallas_call(functools.partial(kernel, room), out_shape=(jax.ShapeDtype...  56.1 us
    slice x1, local copies, waits for them, and re-layouts, shards(): over[0, 0] > 0  1.2 us

profile of v2, /device:TPU:1, one launch (start us, length us, event | category | flops | bytes accessed | tf_op | source)
XLA Modules:
  0.0 58.8 jit_solution(4887091698173422364)
XLA Ops:
  0.0 56.1 %shard_map.39 = (f32[4,128]{1,0:T(4,128)}, f32[8,128]{1,0:T(8,128)}) custom-call(bf16[512,768]{1,0:T(8,128)(2,1)} %emb_hbm.1, s32[4,128]{1,0:T(4,128)} %bitcast.5, s32[4,128]{1,0:T(4,128)} %bitcast.7), custom_call_target="tpu_custom_call" | custom-call | tf_op jit(solution)/shard_map/pallas_call | solution.py:283
  56.1 1.2 %slice.3 = f32[1,1]{1,0:T(1,128)} slice(f32[8,128]{1,0:T(8,128)} %get-tuple-element.23), slice={[0:1], [0:1]} | slice | bytes 8 | tf_op jit(solution)/shard_map/slice | solution.py:328
  57.3 0.0 copy-start
  58.0 0.0 copy-done
  58.0 0.2 conditional.1
  58.2 0.6 copy.10
Async XLA Ops:
  57.3 0.7 %copy-start = (f32[4,128]{1,0:T(4,128)S(1)}, f32[4,128]{1,0:T(4,128)}, u32[]{:S(2)}) copy-start(f32[4,128]{1,0:T(4,128)} %get-tuple-element.24) | copy-start | bytes 6148

commit v3 on v2

v3 whole, which is shorter than its diff:
```python
import functools

import jax
import jax.numpy as jnp
from jax import lax
from jax.experimental import pallas as pl
from jax.experimental.pallas import tpu as pltpu
from jax.sharding import PartitionSpec as P

MESH = pl.DeviceIdType.MESH
CLUSTERS = 256
CAP = 4
WIDTH = 768
ROWS_DEV = 512
PLANES = 8
PEERS = 32
SLOTS = PEERS * CAP
BLOCKS = ROWS_DEV // 128
ROOM = 80
EMPTY = float(1 << 17)
GROUPS = ((0,), (1, 7), (2, 6), (3, 5), (4,))
ORDER = (1, 7, 2, 6, 3, 5, 4)
epsilon = 1e-06


def place():
    row = lax.axis_index("loader")
    y = lax.axis_index("split")
    return lax.div(row, 8), y, lax.rem(lax.div(row, 2), 4), lax.rem(row, 2)


def device(z, y, x, c):
    return ((z * 4 + x) * 2 + c, y)


def across(here, s):
    z, y, x, c = here
    return device(lax.rem(z + s, PLANES), y, x, c)


def within(here, j, sign):
    z, y, x, c = here
    dy, dx, dc = j % 4, j // 4 % 4, j // 16
    return device(
        z,
        lax.rem(y + (4 + sign * dy) % 4, 4),
        lax.rem(x + (4 + sign * dx) % 4, 4),
        lax.rem(c + dc, 2),
    )


def hops(j):
    return min(j % 4, 4 - j % 4) + min(j // 4 % 4, 4 - j // 4 % 4)


FAR_FIRST = sorted(range(1, PEERS), key=lambda j: -hops(j))


def send(src, dst, sent, landed, to):
    return pltpu.make_async_remote_copy(
        src_ref=src,
        dst_ref=dst,
        send_sem=sent,
        recv_sem=landed,
        device_id=to,
        device_id_type=MESH,
    )


def product(a, b):
    return lax.dot_general(
        a, b, (((1,), (1,)), ((), ())), preferred_element_type=jnp.float32
    )


def iota(shape, dim):
    return lax.broadcasted_iota(jnp.int32, shape, dim)


def own_lanes(tiles_ref):
    group = iota((PLANES, SLOTS), 1) // CAP
    total = jnp.zeros((PLANES, SLOTS), jnp.float32)
    for j in range(PEERS):
        total = jnp.where(group == j, tiles_ref[j], total)
    return total


def kernel(
    room, emb_hbm, cid_hbm, rank_hbm, out_ref, flag_ref,
    raw, cid_ref, rank_ref, unit, meta_out, meta_in, rows_out, rows_in, dense, arrived, members,
    ranks_out, ranks_in, best_out, best_in, back_out, back_in,
    raw_sem, meta_sent, meta_landed, rows_sent, rows_landed, dense_sent, dense_landed,
    ranks_sent, ranks_landed, best_sent, best_landed, back_sent, back_landed,
):
    here = place()
    z, y, x, c = here
    load_cid = pltpu.make_async_copy(cid_hbm, cid_ref, raw_sem.at[BLOCKS])
    load_cid.start()
    loads = [
        pltpu.make_async_copy(
            emb_hbm.at[pl.ds(b * 128, 128)], raw.at[pl.ds(b * 128, 128)], raw_sem.at[b]
        )
        for b in range(BLOCKS)
    ]
    for load in loads:
        load.start()
    load_rank = pltpu.make_async_copy(rank_hbm, rank_ref, raw_sem.at[BLOCKS + 1])
    load_rank.start()
    barrier = pltpu.get_barrier_semaphore()
    for s in (4, 3, 5, 2, 6, 1, 7):
        pl.semaphore_signal(barrier, inc=1, device_id=across(here, s), device_id_type=MESH)
    for j in FAR_FIRST:
        pl.semaphore_signal(barrier, inc=1, device_id=within(here, j, 1), device_id_type=MESH)

    load_cid.wait()
    cid = cid_ref[...]
    owner = cid & (PEERS - 1)
    step = ((cid >> 5) - z) & (PLANES - 1)
    turned = jnp.concatenate([cid, step], axis=0).T
    before = iota((128, 128), 0) < iota((128, 128), 1)
    pack_rows, over = [], jnp.zeros((1, 128), jnp.float32)
    for b in range(BLOCKS):
        along = jnp.zeros((128, 128), jnp.float32)
        for a in range(b + 1):
            aside = turned[:, BLOCKS + a : BLOCKS + a + 1] == step[b : b + 1]
            along += jnp.where(aside & before if a == b else aside, 1.0, 0.0)
        count = jnp.sum(along, axis=0, keepdims=True).astype(jnp.int32)
        pack_rows.append(jnp.where(count < room, step[b : b + 1] * SLOTS + count, -1))
        over = jnp.maximum(over, jnp.where(count < room, 0.0, 2 * EMPTY))
    pack = jnp.concatenate(pack_rows, axis=1)
    for b in range(BLOCKS):
        loads[b].wait()
        values = raw[b * 128 : (b + 1) * 128].astype(jnp.float32)
        scale = lax.rsqrt(jnp.sum(values * values, axis=1, keepdims=True) + epsilon)
        unit[b * 128 : (b + 1) * 128] = (values * scale).astype(jnp.bfloat16)

    rows = {
        s: send(rows_out.at[s], rows_in.at[s], rows_sent.at[s], rows_landed.at[s], across(here, s))
        for s in range(1, PLANES)
    }
    metas = {
        s: send(meta_out.at[s], meta_in.at[s], meta_sent.at[s], meta_landed.at[s], across(here, s))
        for s in range(1, PLANES)
    }

    def gather_rows(group):
        chosen = jnp.concatenate(
            [jnp.where(pack == s * SLOTS + iota((room, ROWS_DEV), 0), 1.0, 0.0) for s in group], axis=0
        ).astype(jnp.bfloat16)
        packed = jnp.dot(chosen, unit[...], preferred_element_type=jnp.float32).astype(jnp.bfloat16)
        for n, s in enumerate(group):
            ref = rows_in if s == 0 else rows_out
            ref[s] = packed[n * room : (n + 1) * room]

    gather_rows((1, 7))
    pl.semaphore_wait(barrier, PLANES - 1 + PEERS - 1)
    rows[1].start()
    rows[7].start()

    peer = (
        (((owner >> 4) - c) & 1) * 16 + (((owner >> 2) - x) & 3) * 4 + ((owner - y) & 3)
    )
    slot_rows = []
    for b in range(BLOCKS):
        same = jnp.zeros((128, 128), jnp.float32)
        for a in range(b + 1):
            alike = turned[:, a : a + 1] == cid[b : b + 1]
            same += jnp.where(alike & before if a == b else alike, 1.0, 0.0)
        position = jnp.sum(same, axis=0, keepdims=True).astype(jnp.int32)
        slot_rows.append(step[b : b + 1] * SLOTS + peer[b : b + 1] * CAP + position)
    over = jnp.max(over, axis=1, keepdims=True)
    slot_turned = jnp.concatenate(slot_rows + pack_rows, axis=0).T
    load_rank.wait()
    rank_turned = (rank_ref[...].astype(jnp.float32) - EMPTY).T
    lane = iota((128, 128), 1)
    for s in range(PLANES):
        name = jnp.zeros((128, 128), jnp.float32)
        rank = jnp.zeros((128, 128), jnp.float32)
        for b in range(BLOCKS):
            slots = slot_turned[:, b : b + 1]
            packs = slot_turned[:, BLOCKS + b : BLOCKS + b + 1]
            name = jnp.where(packs == s * SLOTS + lane, (slots - (s * SLOTS - 1)).astype(jnp.float32), name)
            rank = jnp.where(slots == s * SLOTS + lane, rank_turned[:, b : b + 1], rank)
        ref = meta_in if s == 0 else meta_out
        ref[s, 0:1] = jnp.sum(name, axis=0, keepdims=True) - 1.0
        ref[s, 1:2] = jnp.sum(rank, axis=0, keepdims=True) + (EMPTY + over)
    for s in ORDER:
        metas[s].start()
    for group in ((2, 6), (3, 5), (4, 0)):
        gather_rows(group)
        for s in group:
            if s:
                rows[s].start()

    others = pl.ds(1, PEERS - 1)

    def spread(s):
        chosen = jnp.where(
            meta_in[s, 0:1, :room] == iota((SLOTS, room), 0).astype(jnp.float32), 1.0, 0.0
        ).astype(jnp.bfloat16)
        placed = jnp.dot(chosen, rows_in[s], preferred_element_type=jnp.float32).astype(jnp.bfloat16)
        dense[s] = placed.reshape(PEERS, CAP, WIDTH)
        arrived[s, 0] = placed[:CAP]
        for j in FAR_FIRST:
            send(dense.at[s, j], arrived.at[s, j], dense_sent.at[s], dense_landed.at[s], within(here, j, 1)).start()

    def all_dense(s):
        return send(dense.at[s, others], arrived.at[s, others], dense_sent.at[s], dense_landed.at[s], within(here, 1, 1))

    all_ranks = send(ranks_in.at[others], ranks_in.at[others], ranks_sent, ranks_landed, within(here, 1, 1))
    all_best = send(best_in.at[others], best_in.at[others], best_sent, best_landed, within(here, 1, 1))

    spread(0)
    for s in ORDER:
        metas[s].wait_recv()
    for s in range(PLANES):
        ranks_out[s : s + 1] = meta_in[s, 1:2]
    ranks_in[0] = ranks_out[...]
    for j in FAR_FIRST:
        send(ranks_out, ranks_in.at[j], ranks_sent, ranks_landed, within(here, j, 1)).start()
    for s in GROUPS[1]:
        rows[s].wait_recv()
        spread(s)

    all_ranks.wait_recv()
    rank_row = own_lanes(ranks_in)
    rank_col = rank_row.T
    highest = jnp.zeros((PLANES, SLOTS), jnp.float32)
    for j in range(PEERS):
        highest = jnp.maximum(highest, ranks_in[j])
    flag_ref[0] = jnp.max(jnp.where(highest >= 2 * EMPTY, 1, 0))

    best = [jnp.full((1, SLOTS), -1.0, jnp.float32)] * PLANES
    seen = []

    def compare(group):
        known = len(seen)
        for s in group:
            all_dense(s).wait_recv()
            members[len(seen) * SLOTS : (len(seen) + 1) * SLOTS] = arrived[s].reshape(SLOTS, WIDTH)
            seen.append(s)
        scores = product(members[known * SLOTS : len(seen) * SLOTS], members[: len(seen) * SLOTS])

        def part(n, k):
            return scores[n * SLOTS : (n + 1) * SLOTS, k * SLOTS : (k + 1) * SLOTS]

        for k, q in enumerate(seen):
            top = jnp.full((SLOTS, SLOTS), -1.0, jnp.float32)
            for n, m in enumerate(group):
                earlier = rank_col[:, m : m + 1] < rank_row[q : q + 1]
                top = jnp.maximum(top, jnp.where(earlier, part(n, k), -1.0))
            best[q] = jnp.maximum(best[q], jnp.max(top, axis=0, keepdims=True))
        for n, q in enumerate(group):
            if known:
                top = jnp.full((SLOTS, SLOTS), -1.0, jnp.float32)
                for k, m in enumerate(seen[:known]):
                    earlier = rank_row[m : m + 1] < rank_col[:, q : q + 1]
                    top = jnp.maximum(top, jnp.where(earlier, part(n, k), -1.0))
                best[q] = jnp.maximum(best[q], jnp.max(top.T, axis=0, keepdims=True))

    compare(GROUPS[0])
    for s in GROUPS[2]:
        rows[s].wait_recv()
        spread(s)
    compare(GROUPS[1])
    for s in GROUPS[3] + GROUPS[4]:
        rows[s].wait_recv()
        spread(s)
    for group in GROUPS[2:]:
        compare(group)

    best_out[...] = jnp.concatenate(best, axis=0)
    for j in FAR_FIRST:
        send(best_out, best_in.at[j], best_sent, best_landed, within(here, j, -1)).start()
    best_in[0] = best_out[...]
    for s in ORDER:
        metas[s].wait_send()
        rows[s].wait_send()
    for s in range(PLANES):
        all_dense(s).wait_send()
    all_ranks.wait_send()
    all_best.wait_recv()
    results = own_lanes(best_in)
    backs = []
    for s in (4, 3, 5, 2, 6, 1, 7):
        back_out[s] = results[s : s + 1]
        back = send(back_out.at[s], back_in.at[s], back_sent.at[s], back_landed.at[s], across(here, PLANES - s))
        back.start()
        backs.append(back)
    back_in[0] = results[0:1]
    all_best.wait_send()
    for back in backs:
        back.wait()
    result_col = jnp.concatenate([back_in[s] for s in range(PLANES)], axis=0).T
    slot = iota((SLOTS, 128), 0)
    for b in range(BLOCKS):
        found = jnp.zeros((SLOTS, 128), jnp.float32)
        for s in range(PLANES):
            found = jnp.where(slot_rows[b] == s * SLOTS + slot, result_col[:, s : s + 1], found)
        out_ref[b : b + 1] = jnp.sum(found, axis=0, keepdims=True)


def exchange(room, number, vmem, embeddings, cluster_ids, ranks):
    dma = pltpu.SemaphoreType.DMA
    return pl.pallas_call(
        functools.partial(kernel, room),
        out_shape=(
            jax.ShapeDtypeStruct((BLOCKS, 128), jnp.float32),
            jax.ShapeDtypeStruct((1,), jnp.int32),
        ),
        in_specs=[
            pl.BlockSpec(memory_space=pltpu.HBM),
            pl.BlockSpec(memory_space=pltpu.HBM),
            pl.BlockSpec(memory_space=pltpu.HBM),
        ],
        out_specs=(pl.BlockSpec(memory_space=pltpu.VMEM), pl.BlockSpec(memory_space=pltpu.SMEM)),
        scratch_shapes=[
            pltpu.VMEM((ROWS_DEV, WIDTH), jnp.bfloat16),
            pltpu.VMEM((BLOCKS, 128), jnp.int32),
            pltpu.VMEM((BLOCKS, 128), jnp.int32),
            pltpu.VMEM((ROWS_DEV, WIDTH), jnp.bfloat16),
            pltpu.VMEM((PLANES, 2, SLOTS), jnp.float32),
            pltpu.VMEM((PLANES, 2, SLOTS), jnp.float32),
            pltpu.VMEM((PLANES, room, WIDTH), jnp.bfloat16),
            pltpu.VMEM((PLANES, room, WIDTH), jnp.bfloat16),
            pltpu.VMEM((PLANES, PEERS, CAP, WIDTH), jnp.bfloat16),
            pltpu.VMEM((PLANES, PEERS, CAP, WIDTH), jnp.bfloat16),
            pltpu.VMEM((PLANES * SLOTS, WIDTH), jnp.bfloat16),
            pltpu.VMEM((PLANES, SLOTS), jnp.float32),
            pltpu.VMEM((PEERS, PLANES, SLOTS), jnp.float32),
            pltpu.VMEM((PLANES, SLOTS), jnp.float32),
            pltpu.VMEM((PEERS, PLANES, SLOTS), jnp.float32),
            pltpu.VMEM((PLANES, 1, SLOTS), jnp.float32),
            pltpu.VMEM((PLANES, 1, SLOTS), jnp.float32),
            dma((BLOCKS + 2,)),
            dma((PLANES,)), dma((PLANES,)),
            dma((PLANES,)), dma((PLANES,)),
            dma((PLANES,)), dma((PLANES,)),
            dma, dma,
            dma, dma,
            dma((PLANES,)), dma((PLANES,)),
        ],
        compiler_params=pltpu.CompilerParams(
            collective_id=number, has_side_effects=True, vmem_limit_bytes=vmem
        ),
    )(embeddings, cluster_ids, ranks)


def shards(embeddings, cluster_ids, ranks):
    given = embeddings, cluster_ids.reshape(BLOCKS, 128), ranks.reshape(BLOCKS, 128)
    nearest, over = exchange(ROOM, 0, 40 << 20, *given)
    nearest = lax.cond(over[0] > 0, lambda best: exchange(SLOTS, 1, 67043328, *given)[0], lambda best: best, nearest)
    return nearest.reshape(ROWS_DEV)


def solution(mesh):
    return jax.shard_map(
        shards,
        mesh=mesh,
        in_specs=(
            P(("loader", "split"), None),
            P(("loader", "split"), None),
            P(("loader", "split")),
        ),
        out_specs=P(("loader", "split")),
        check_vma=False,
    )
```

time: 59 us -> 52.6 us (0.89)
  Pallas kernels: 56.1 us -> 51.1 us
  local copies, waits for them, and re-layouts: 1.8 us -> 0.58 us
    pallas_call x1, Pallas kernels: 56.1 us -> 51.1 us  [exchange(): pl.pallas_call(functools.partial(kernel, room), out_shape=(jax.ShapeDtype...]
    slice x1 -> x0, local copies, waits for them, and re-layouts: 1.2 us -> none  [shards(): over[0, 0] > 0]
where the time goes in v3:
time: 52.6 us; the launch traced here: 52.5 us
  Pallas kernels  51.1 us (97%)
  between operations  0.64 us (1%)
  local copies, waits for them, and re-layouts  0.58 us (1%)
    pallas_call x1, Pallas kernels, exchange(): pl.pallas_call(functools.partial(kernel, room), out_shape=(jax.ShapeDtype...  51.1 us

profile of v3, /device:TPU:1, one launch (start us, length us, event | category | flops | bytes accessed | tf_op | source)
XLA Modules:
  0.0 52.5 jit_solution(2815208223654735672)
XLA Ops:
  0.0 51.1 %shard_map.39 = (f32[4,128]{1,0:T(4,128)S(1)}, s32[1]{0:T(128)}) custom-call(bf16[512,768]{1,0:T(8,128)(2,1)} %emb_hbm.1, s32[4,128]{1,0:T(4,128)} %bitcast.2.cid_hbm, s32[4,128]{1,0:T(4,128)} %bitcast.3.rank_hbm), custom_call_target="tpu_custom_call" | custom-call | tf_op jit(solution)/shard_map/pallas_call | solution.py:305
  51.8 0.2 conditional.1
  51.9 0.6 %copy.10 = f32[512]{0:T(512)} copy(f32[512]{0:T(512)S(1)} %get-tuple-element.25) | data formatting | bytes 4096

commit v4 on v3

v4 whole, which is shorter than its diff:
```python
import functools

import jax
import jax.numpy as jnp
from jax import lax
from jax.experimental import pallas as pl
from jax.experimental.pallas import tpu as pltpu
from jax.sharding import PartitionSpec as P

MESH = pl.DeviceIdType.MESH
scope = jax.named_scope
CLUSTERS = 256
CAP = 4
WIDTH = 768
ROWS_DEV = 512
PLANES = 8
PEERS = 32
SLOTS = PEERS * CAP
BLOCKS = ROWS_DEV // 128
ROOM = 80
EMPTY = float(1 << 17)
GROUPS = ((0,), (1, 7), (2, 6), (3, 5), (4,))
ORDER = sum(GROUPS[1:], ())
epsilon = 1e-06


def place():
    row = lax.axis_index("loader")
    y = lax.axis_index("split")
    return lax.div(row, 8), y, lax.rem(lax.div(row, 2), 4), lax.rem(row, 2)


def device(z, y, x, c):
    return ((z * 4 + x) * 2 + c, y)


def across(here, s):
    z, y, x, c = here
    return device(lax.rem(z + s, PLANES), y, x, c)


def within(here, j, sign):
    z, y, x, c = here
    dy, dx, dc = j % 4, j // 4 % 4, j // 16
    return device(
        z,
        lax.rem(y + (4 + sign * dy) % 4, 4),
        lax.rem(x + (4 + sign * dx) % 4, 4),
        lax.rem(c + dc, 2),
    )


def hops(j):
    return min(j % 4, 4 - j % 4) + min(j // 4 % 4, 4 - j // 4 % 4)


FAR_FIRST = sorted(range(1, PEERS), key=lambda j: -hops(j))


def send(src, dst, sent, landed, to):
    return pltpu.make_async_remote_copy(
        src_ref=src,
        dst_ref=dst,
        send_sem=sent,
        recv_sem=landed,
        device_id=to,
        device_id_type=MESH,
    )


def product(a, b):
    return lax.dot_general(
        a, b, (((1,), (1,)), ((), ())), preferred_element_type=jnp.float32
    )


def iota(shape, dim):
    return lax.broadcasted_iota(jnp.int32, shape, dim)


def own_lanes(tiles_ref):
    group = iota((PLANES, SLOTS), 1) // CAP
    total = jnp.zeros((PLANES, SLOTS), jnp.float32)
    for j in range(PEERS):
        total = jnp.where(group == j, tiles_ref[j], total)
    return total


def kernel(
    room, emb_hbm, cid_hbm, rank_hbm, out_ref, flag_ref,
    raw, cid_ref, rank_ref, unit, meta_out, meta_in, rows_out, rows_in, dense, arrived, members,
    ranks_out, ranks_in, best_out, best_in, back_out, back_in,
    raw_sem, meta_sent, meta_landed, rows_sent, rows_landed, dense_sent, dense_landed,
    ranks_sent, ranks_landed, best_sent, best_landed, back_sent, back_landed,
):
    here = place()
    z, y, x, c = here
    load_cid = pltpu.make_async_copy(cid_hbm, cid_ref, raw_sem.at[BLOCKS])
    load_cid.start()
    loads = [
        pltpu.make_async_copy(
            emb_hbm.at[pl.ds(b * 128, 128)], raw.at[pl.ds(b * 128, 128)], raw_sem.at[b]
        )
        for b in range(BLOCKS)
    ]
    for load in loads:
        load.start()
    load_rank = pltpu.make_async_copy(rank_hbm, rank_ref, raw_sem.at[BLOCKS + 1])
    load_rank.start()
    with scope("greet"):
        barrier = pltpu.get_barrier_semaphore()
        for s in (4, 3, 5, 2, 6, 1, 7):
            pl.semaphore_signal(barrier, inc=1, device_id=across(here, s), device_id_type=MESH)
        for j in FAR_FIRST:
            pl.semaphore_signal(barrier, inc=1, device_id=within(here, j, 1), device_id_type=MESH)

    with scope("count"):
        load_cid.wait()
        cid = cid_ref[...]
        owner = cid & (PEERS - 1)
        step = ((cid >> 5) - z) & (PLANES - 1)
        turned = jnp.concatenate([cid, step], axis=0).T
        before = iota((128, 128), 0) < iota((128, 128), 1)
        pack_rows, over = [], jnp.zeros((1, 128), jnp.float32)
        for b in range(BLOCKS):
            along = jnp.zeros((128, 128), jnp.float32)
            for a in range(b + 1):
                aside = turned[:, BLOCKS + a : BLOCKS + a + 1] == step[b : b + 1]
                along += jnp.where(aside & before if a == b else aside, 1.0, 0.0)
            count = jnp.sum(along, axis=0, keepdims=True).astype(jnp.int32)
            pack_rows.append(jnp.where(count < room, step[b : b + 1] * SLOTS + count, -1))
            over = jnp.maximum(over, jnp.where(count < room, 0.0, 2 * EMPTY))
        pack = jnp.concatenate(pack_rows, axis=1)
    with scope("norm"):
        for b in range(BLOCKS):
            loads[b].wait()
            values = raw[b * 128 : (b + 1) * 128].astype(jnp.float32)
            scale = lax.rsqrt(jnp.sum(values * values, axis=1, keepdims=True) + epsilon)
            unit[b * 128 : (b + 1) * 128] = (values * scale).astype(jnp.bfloat16)

    rows = {
        s: send(rows_out.at[s], rows_in.at[s], rows_sent.at[s], rows_landed.at[s], across(here, s))
        for s in range(1, PLANES)
    }
    metas = {
        s: send(meta_out.at[s], meta_in.at[s], meta_sent.at[s], meta_landed.at[s], across(here, s))
        for s in range(1, PLANES)
    }

    def gather_rows(group):
        chosen = jnp.concatenate(
            [jnp.where(pack == s * SLOTS + iota((room, ROWS_DEV), 0), 1.0, 0.0) for s in group], axis=0
        ).astype(jnp.bfloat16)
        packed = jnp.dot(chosen, unit[...], preferred_element_type=jnp.float32).astype(jnp.bfloat16)
        for n, s in enumerate(group):
            ref = rows_in if s == 0 else rows_out
            ref[s] = packed[n * room : (n + 1) * room]

    with scope("pack"):
        gather_rows(GROUPS[1])
    with scope("barrier_wait"):
        pl.semaphore_wait(barrier, PLANES - 1 + PEERS - 1)
    for s in GROUPS[1]:
        rows[s].start()

    with scope("slots"):
        peer = (
            (((owner >> 4) - c) & 1) * 16 + (((owner >> 2) - x) & 3) * 4 + ((owner - y) & 3)
        )
        slot_rows = []
        for b in range(BLOCKS):
            same = jnp.zeros((128, 128), jnp.float32)
            for a in range(b + 1):
                alike = turned[:, a : a + 1] == cid[b : b + 1]
                same += jnp.where(alike & before if a == b else alike, 1.0, 0.0)
            position = jnp.sum(same, axis=0, keepdims=True).astype(jnp.int32)
            slot_rows.append(step[b : b + 1] * SLOTS + peer[b : b + 1] * CAP + position)
        over = jnp.max(over, axis=1, keepdims=True)
        slot_turned = jnp.concatenate(slot_rows + pack_rows, axis=0).T
        load_rank.wait()
        rank_turned = (rank_ref[...].astype(jnp.float32) - EMPTY).T
        lane = iota((128, 128), 1)
        for s in range(PLANES):
            name = jnp.zeros((128, 128), jnp.float32)
            rank = jnp.zeros((128, 128), jnp.float32)
            for b in range(BLOCKS):
                slots = slot_turned[:, b : b + 1]
                packs = slot_turned[:, BLOCKS + b : BLOCKS + b + 1]
                name = jnp.where(packs == s * SLOTS + lane, (slots - (s * SLOTS - 1)).astype(jnp.float32), name)
                rank = jnp.where(slots == s * SLOTS + lane, rank_turned[:, b : b + 1], rank)
            ref = meta_in if s == 0 else meta_out
            ref[s, 0:1] = jnp.sum(name, axis=0, keepdims=True) - 1.0
            ref[s, 1:2] = jnp.sum(rank, axis=0, keepdims=True) + (EMPTY + over)
    for s in ORDER:
        metas[s].start()
    with scope("pack_rest"):
        for group in GROUPS[2:] + GROUPS[:1]:
            gather_rows(group)
            for s in group:
                if s:
                    rows[s].start()

    others = pl.ds(1, PEERS - 1)

    def spread(s):
        with scope(f"place#s={s}"):
            chosen = jnp.where(
                meta_in[s, 0:1, :room] == iota((SLOTS, room), 0).astype(jnp.float32), 1.0, 0.0
            ).astype(jnp.bfloat16)
            placed = jnp.dot(chosen, rows_in[s], preferred_element_type=jnp.float32).astype(jnp.bfloat16)
            dense[s] = placed.reshape(PEERS, CAP, WIDTH)
            arrived[s, 0] = placed[:CAP]
        with scope(f"deliver#s={s}"):
            for j in FAR_FIRST:
                send(dense.at[s, j], arrived.at[s, j], dense_sent.at[s], dense_landed.at[s], within(here, j, 1)).start()

    def all_dense(s):
        return send(dense.at[s, others], arrived.at[s, others], dense_sent.at[s], dense_landed.at[s], within(here, 1, 1))

    all_ranks = send(ranks_in.at[others], ranks_in.at[others], ranks_sent, ranks_landed, within(here, 1, 1))
    all_best = send(best_in.at[others], best_in.at[others], best_sent, best_landed, within(here, 1, 1))

    spread(0)
    for s in GROUPS[1]:
        with scope(f"rows_wait#s={s}"):
            metas[s].wait_recv()
            rows[s].wait_recv()
        spread(s)
    with scope("meta_wait"):
        for s in ORDER[len(GROUPS[1]) :]:
            metas[s].wait_recv()
    for s in range(PLANES):
        ranks_out[s : s + 1] = meta_in[s, 1:2]
    ranks_in[0] = ranks_out[...]
    for j in FAR_FIRST:
        send(ranks_out, ranks_in.at[j], ranks_sent, ranks_landed, within(here, j, 1)).start()

    for s in GROUPS[2]:
        with scope(f"rows_wait#s={s}"):
            rows[s].wait_recv()
        spread(s)
    with scope("ranks_wait"):
        all_ranks.wait_recv()
    rank_row = own_lanes(ranks_in)
    rank_col = rank_row.T
    highest = jnp.zeros((PLANES, SLOTS), jnp.float32)
    for j in range(PEERS):
        highest = jnp.maximum(highest, ranks_in[j])
    flag_ref[0] = jnp.max(jnp.where(highest >= 2 * EMPTY, 1, 0))

    best = [jnp.full((1, SLOTS), -1.0, jnp.float32)] * PLANES
    seen = []

    def compare(group):
        known = len(seen)
        for s in group:
            with scope(f"dense_wait#s={s}"):
                all_dense(s).wait_recv()
            members[len(seen) * SLOTS : (len(seen) + 1) * SLOTS] = arrived[s].reshape(SLOTS, WIDTH)
            seen.append(s)
        with scope(f"scores#n={len(seen)}"):
            scores = product(members[known * SLOTS : len(seen) * SLOTS], members[: len(seen) * SLOTS])

            def part(n, k):
                return scores[n * SLOTS : (n + 1) * SLOTS, k * SLOTS : (k + 1) * SLOTS]

            for k, q in enumerate(seen):
                top = jnp.full((SLOTS, SLOTS), -1.0, jnp.float32)
                for n, m in enumerate(group):
                    earlier = rank_col[:, m : m + 1] < rank_row[q : q + 1]
                    top = jnp.maximum(top, jnp.where(earlier, part(n, k), -1.0))
                best[q] = jnp.maximum(best[q], jnp.max(top, axis=0, keepdims=True))
            for n, q in enumerate(group):
                if known:
                    top = jnp.full((SLOTS, SLOTS), -1.0, jnp.float32)
                    for k, m in enumerate(seen[:known]):
                        earlier = rank_row[m : m + 1] < rank_col[:, q : q + 1]
                        top = jnp.maximum(top, jnp.where(earlier, part(n, k), -1.0))
                    best[q] = jnp.maximum(best[q], jnp.max(top.T, axis=0, keepdims=True))

    compare(GROUPS[0])
    compare(GROUPS[1])
    for s in GROUPS[3] + GROUPS[4]:
        with scope(f"rows_wait#s={s}"):
            rows[s].wait_recv()
        spread(s)
    compare(GROUPS[2])
    for s in GROUPS[3] + GROUPS[4]:
        compare((s,))

    lanes, peers = iota((PEERS, SLOTS), 1), iota((PEERS, SLOTS), 0)
    with scope("answer"):
        answers = jnp.zeros((PEERS, SLOTS), jnp.float32)
        for s in range(PLANES):
            line = jnp.broadcast_to(best[s], (PEERS, SLOTS))
            picked = jnp.take_along_axis(line, CAP * peers + (lanes & (CAP - 1)), axis=1)
            answers = jnp.where(lanes // CAP == s, picked, answers)
        best_out[...] = answers.reshape(PEERS, 1, SLOTS)
        for j in FAR_FIRST:
            send(best_out.at[j], best_in.at[j], best_sent, best_landed, within(here, j, -1)).start()
    best_in[0] = best_out[0]
    for s in ORDER:
        metas[s].wait_send()
        rows[s].wait_send()
    for s in range(PLANES):
        all_dense(s).wait_send()
    all_ranks.wait_send()
    with scope("best_wait"):
        all_best.wait_recv()
    with scope("back"):
        answers = best_in[...].reshape(PEERS, SLOTS)
        backs = []
        for s in (4, 3, 5, 2, 6, 1, 7, 0):
            picked = jnp.take_along_axis(answers, CAP * s + (lanes & (CAP - 1)), axis=1)
            line = jnp.sum(jnp.where(lanes // CAP == peers, picked, 0.0), axis=0, keepdims=True)
            if s == 0:
                back_in[0] = line
                continue
            back_out[s] = line
            back = send(back_out.at[s], back_in.at[s], back_sent.at[s], back_landed.at[s], across(here, PLANES - s))
            back.start()
            backs.append(back)
    all_best.wait_send()
    with scope("back_wait"):
        for back in backs:
            back.wait()
    with scope("final"):
        slot = jnp.concatenate(slot_rows * 2, axis=0)
        found = jnp.zeros((2 * BLOCKS, 128), jnp.float32)
        for s in range(PLANES):
            row = jnp.broadcast_to(back_in[s], (2 * BLOCKS, SLOTS))
            picked = jnp.take_along_axis(row, slot & (SLOTS - 1), axis=1)
            found = jnp.where(slot >> 7 == s, picked, found)
        out_ref[...] = found[:BLOCKS]


def exchange(room, number, vmem, embeddings, cluster_ids, ranks):
    dma = pltpu.SemaphoreType.DMA
    return pl.pallas_call(
        functools.partial(kernel, room),
        out_shape=(
            jax.ShapeDtypeStruct((BLOCKS, 128), jnp.float32),
            jax.ShapeDtypeStruct((1,), jnp.int32),
        ),
        in_specs=[
            pl.BlockSpec(memory_space=pltpu.HBM),
            pl.BlockSpec(memory_space=pltpu.HBM),
            pl.BlockSpec(memory_space=pltpu.HBM),
        ],
        out_specs=(pl.BlockSpec(memory_space=pltpu.VMEM), pl.BlockSpec(memory_space=pltpu.SMEM)),
        scratch_shapes=[
            pltpu.VMEM((ROWS_DEV, WIDTH), jnp.bfloat16),
            pltpu.VMEM((BLOCKS, 128), jnp.int32),
            pltpu.VMEM((BLOCKS, 128), jnp.int32),
            pltpu.VMEM((ROWS_DEV, WIDTH), jnp.bfloat16),
            pltpu.VMEM((PLANES, 2, SLOTS), jnp.float32),
            pltpu.VMEM((PLANES, 2, SLOTS), jnp.float32),
            pltpu.VMEM((PLANES, room, WIDTH), jnp.bfloat16),
            pltpu.VMEM((PLANES, room, WIDTH), jnp.bfloat16),
            pltpu.VMEM((PLANES, PEERS, CAP, WIDTH), jnp.bfloat16),
            pltpu.VMEM((PLANES, PEERS, CAP, WIDTH), jnp.bfloat16),
            pltpu.VMEM((PLANES * SLOTS, WIDTH), jnp.bfloat16),
            pltpu.VMEM((PLANES, SLOTS), jnp.float32),
            pltpu.VMEM((PEERS, PLANES, SLOTS), jnp.float32),
            pltpu.VMEM((PEERS, 1, SLOTS), jnp.float32),
            pltpu.VMEM((PEERS, 1, SLOTS), jnp.float32),
            pltpu.VMEM((PLANES, 1, SLOTS), jnp.float32),
            pltpu.VMEM((PLANES, 1, SLOTS), jnp.float32),
            dma((BLOCKS + 2,)),
            dma((PLANES,)), dma((PLANES,)),
            dma((PLANES,)), dma((PLANES,)),
            dma((PLANES,)), dma((PLANES,)),
            dma, dma,
            dma, dma,
            dma((PLANES,)), dma((PLANES,)),
        ],
        compiler_params=pltpu.CompilerParams(
            collective_id=number, has_side_effects=True, vmem_limit_bytes=vmem
        ),
    )(embeddings, cluster_ids, ranks)


def shards(embeddings, cluster_ids, ranks):
    given = embeddings, cluster_ids.reshape(BLOCKS, 128), ranks.reshape(BLOCKS, 128)
    nearest, over = exchange(ROOM, 0, 40 << 20, *given)
    nearest = lax.switch(over[0], (lambda best: best, lambda best: exchange(SLOTS, 1, 67043328, *given)[0]), nearest)
    return nearest.reshape(ROWS_DEV)


def solution(mesh):
    return jax.shard_map(
        shards,
        mesh=mesh,
        in_specs=(
            P(("loader", "split"), None),
            P(("loader", "split"), None),
            P(("loader", "split")),
        ),
        out_specs=P(("loader", "split")),
        check_vma=False,
    )
```

time: 52.6 us -> 52.2 us (level)
  no operation moved by 1% of the time
where the time goes in v4:
time: 52.2 us; the launch traced here: 52.1 us
  Pallas kernels  50.7 us (97%)
  between operations  0.64 us (1%)
  local copies, waits for them, and re-layouts  0.58 us (1%)
    pallas_call x1, Pallas kernels, exchange(): pl.pallas_call(functools.partial(kernel, room), out_shape=(jax.ShapeDtype...  50.7 us

profile of v4, /device:TPU:1, one launch (start us, length us, event | category | flops | bytes accessed | tf_op | source)
XLA Modules:
  0.0 52.1 jit_solution(15618638559440981473)
XLA Ops:
  0.0 50.7 %shard_map.39 = (f32[4,128]{1,0:T(4,128)S(1)}, s32[1]{0:T(128)}) custom-call(bf16[512,768]{1,0:T(8,128)(2,1)} %emb_hbm.1, s32[4,128]{1,0:T(4,128)} %bitcast.2.cid_hbm, s32[4,128]{1,0:T(4,128)} %bitcast.3.rank_hbm), custom_call_target="tpu_custom_call" | custom-call | tf_op jit(solution)/shard_map/pallas_call | solution.py:339
  51.3 0.2 conditional.1
  51.5 0.6 %copy.10 = f32[512]{0:T(512)} copy(f32[512]{0:T(512)S(1)} %get-tuple-element.25) | data formatting | bytes 4096

commit v5 on v4

--- a/solution.py
+++ b/solution.py
@@ -19,7 +19,7 @@
 BLOCKS = ROWS_DEV // 128
 ROOM = 80
 EMPTY = float(1 << 17)
-GROUPS = ((0,), (1, 7), (2, 6), (3, 5), (4,))
+GROUPS = ((0,), (1, 7), (2, 6), (5, 3), (4,))
 ORDER = sum(GROUPS[1:], ())
 epsilon = 1e-06
 
@@ -54,7 +54,12 @@
     return min(j % 4, 4 - j % 4) + min(j // 4 % 4, 4 - j // 4 % 4)
 
 
+FIRST = [(z, y, x) for z in range(3) for y in range(4) for x in range(4) if z + min(y, 4 - y) + min(x, 4 - x) <= 2]
 FAR_FIRST = sorted(range(1, PEERS), key=lambda j: -hops(j))
+
+
+def is_first(z, y, x):
+    return z + jnp.minimum(y, 4 - y) + jnp.minimum(x, 4 - x) <= 2
 
 
 def send(src, dst, sent, landed, to):
@@ -89,9 +94,9 @@
 def kernel(
     room, emb_hbm, cid_hbm, rank_hbm, out_ref, flag_ref,
     raw, cid_ref, rank_ref, unit, meta_out, meta_in, rows_out, rows_in, dense, arrived, members,
-    ranks_out, ranks_in, best_out, best_in, back_out, back_in,
+    ranks_out, ranks_in, best_out, best_rows, best_in, far_in, back_out, back_in,
     raw_sem, meta_sent, meta_landed, rows_sent, rows_landed, dense_sent, dense_landed,
-    ranks_sent, ranks_landed, best_sent, best_landed, back_sent, back_landed,
+    ranks_sent, ranks_landed, best_sent, best_landed, far_sent, far_landed, back_sent, back_landed,
 ):
     here = place()
     z, y, x, c = here
@@ -289,7 +294,15 @@
         compare((s,))
 
     lanes, peers = iota((PEERS, SLOTS), 1), iota((PEERS, SLOTS), 0)
+    straight = []
+    for n, (a, b, d, e) in enumerate((*chip, core) for chip in FIRST for core in (1, 0)):
+        up, j = lax.rem(z - a + PLANES, PLANES), lax.rem(c + e, 2) * 16 + lax.rem(x - d + 4, 4) * 4 + lax.rem(y - b + 4, 4)
+        straight.append((up, send(best_rows.at[up], far_in.at[up, j], far_sent.at[n], far_landed, device(a, b, d, e))))
     with scope("answer"):
+        for s in range(PLANES):
+            best_rows[s] = best[s]
+        for up, copy in straight:
+            pl.when(up != 0)(copy.start)
         answers = jnp.zeros((PEERS, SLOTS), jnp.float32)
         for s in range(PLANES):
             line = jnp.broadcast_to(best[s], (PEERS, SLOTS))
@@ -318,12 +331,31 @@
                 continue
             back_out[s] = line
             back = send(back_out.at[s], back_in.at[s], back_sent.at[s], back_landed.at[s], across(here, PLANES - s))
-            back.start()
-            backs.append(back)
+            wanted = jnp.logical_not(is_first(lax.rem(z + PLANES - s, PLANES), y, x))
+            pl.when(wanted)(back.start)
+            backs.append((wanted, back))
     all_best.wait_send()
-    with scope("back_wait"):
-        for back in backs:
-            back.wait()
+    for up, copy in straight:
+        pl.when(up != 0)(copy.wait_send)
+    for wanted, back in backs:
+        pl.when(wanted)(back.wait_send)
+    first = is_first(z, y, x)
+
+    @pl.when(jnp.logical_not(first))
+    def _():
+        with scope("back_wait"):
+            for _, back in backs:
+                back.wait_recv()
+
+    @pl.when(first)
+    def _():
+        steps = far_in.at[pl.ds(1, PLANES - 1)]
+        with scope("far_wait"):
+            send(steps, steps, far_sent.at[0], far_landed, across(here, 1)).wait_recv()
+        for s in range(1, PLANES):
+            tiles = far_in[s].reshape(PEERS, SLOTS)
+            back_in[s] = jnp.sum(jnp.where(lanes // CAP == peers, tiles, 0.0), axis=0, keepdims=True)
+
     with scope("final"):
         slot = jnp.concatenate(slot_rows * 2, axis=0)
         found = jnp.zeros((2 * BLOCKS, 128), jnp.float32)
@@ -363,7 +395,9 @@
             pltpu.VMEM((PLANES, SLOTS), jnp.float32),
             pltpu.VMEM((PEERS, PLANES, SLOTS), jnp.float32),
             pltpu.VMEM((PEERS, 1, SLOTS), jnp.float32),
+            pltpu.VMEM((PLANES, 1, SLOTS), jnp.float32),
             pltpu.VMEM((PEERS, 1, SLOTS), jnp.float32),
+            pltpu.VMEM((PLANES, PEERS, 1, SLOTS), jnp.float32),
             pltpu.VMEM((PLANES, 1, SLOTS), jnp.float32),
             pltpu.VMEM((PLANES, 1, SLOTS), jnp.float32),
             dma((BLOCKS + 2,)),
@@ -372,6 +406,7 @@
             dma((PLANES,)), dma((PLANES,)),
             dma, dma,
             dma, dma,
+            dma((2 * len(FIRST),)), dma,
             dma((PLANES,)), dma((PLANES,)),
         ],
         compiler_params=pltpu.CompilerParams(

time: 52.2 us -> 50.6 us (0.969)
  Pallas kernels: 50.7 us -> 49.1 us
    pallas_call x1, Pallas kernels: 50.7 us -> 49.1 us  [exchange(): pl.pallas_call(functools.partial(kernel, room), out_shape=(jax.ShapeDtype...]
where the time goes in v5:
time: 50.6 us; the launch traced here: 50.5 us
  Pallas kernels  49.1 us (97%)
  between operations  0.64 us (1%)
  local copies, waits for them, and re-layouts  0.58 us (1%)
    pallas_call x1, Pallas kernels, exchange(): pl.pallas_call(functools.partial(kernel, room), out_shape=(jax.ShapeDtype...  49.1 us

profile of v5, /device:TPU:1, one launch (start us, length us, event | category | flops | bytes accessed | tf_op | source)
XLA Modules:
  0.0 50.5 jit_solution(6589845498128735239)
XLA Ops:
  0.0 49.1 %shard_map.39 = (f32[4,128]{1,0:T(4,128)S(1)}, s32[1]{0:T(128)}) custom-call(bf16[512,768]{1,0:T(8,128)(2,1)} %emb_hbm.1, s32[4,128]{1,0:T(4,128)} %bitcast.2.cid_hbm, s32[4,128]{1,0:T(4,128)} %bitcast.3.rank_hbm), custom_call_target="tpu_custom_call" | custom-call | tf_op jit(solution)/shard_map/pallas_call | solution.py:371
  49.7 0.2 conditional.1
  49.9 0.6 %copy.10 = f32[512]{0:T(512)} copy(f32[512]{0:T(512)S(1)} %get-tuple-element.25) | data formatting | bytes 4096

commit v6 on v5

--- a/solution.py
+++ b/solution.py
@@ -55,6 +55,8 @@
 
 
 FIRST = [(z, y, x) for z in range(3) for y in range(4) for x in range(4) if z + min(y, 4 - y) + min(x, 4 - x) <= 2]
+BESIDE = (1, 3, 4, 12, 16)
+ROUNDS = ((1, 3), (4, 12), (4, 12), (16,))
 FAR_FIRST = sorted(range(1, PEERS), key=lambda j: -hops(j))
 
 
@@ -96,7 +98,7 @@
     raw, cid_ref, rank_ref, unit, meta_out, meta_in, rows_out, rows_in, dense, arrived, members,
     ranks_out, ranks_in, best_out, best_rows, best_in, far_in, back_out, back_in,
     raw_sem, meta_sent, meta_landed, rows_sent, rows_landed, dense_sent, dense_landed,
-    ranks_sent, ranks_landed, best_sent, best_landed, far_sent, far_landed, back_sent, back_landed,
+    ranks_sent, ranks_landed, best_sent, best_landed, far_sent, far_landed, back_sent, back_landed, met,
 ):
     here = place()
     z, y, x, c = here
@@ -116,8 +118,16 @@
         barrier = pltpu.get_barrier_semaphore()
         for s in (4, 3, 5, 2, 6, 1, 7):
             pl.semaphore_signal(barrier, inc=1, device_id=across(here, s), device_id_type=MESH)
-        for j in FAR_FIRST:
+        for j in BESIDE:
             pl.semaphore_signal(barrier, inc=1, device_id=within(here, j, 1), device_id_type=MESH)
+
+    def tell(n):
+        for j in ROUNDS[n]:
+            pl.semaphore_signal(met.at[n], inc=1, device_id=within(here, j, 1), device_id_type=MESH)
+
+    def hear(n):
+        with scope(f"hear#n={n}"):
+            pl.semaphore_wait(met.at[n], len(ROUNDS[n]))
 
     with scope("count"):
         load_cid.wait()
@@ -164,9 +174,10 @@
     with scope("pack"):
         gather_rows(GROUPS[1])
     with scope("barrier_wait"):
-        pl.semaphore_wait(barrier, PLANES - 1 + PEERS - 1)
+        pl.semaphore_wait(barrier, PLANES - 1 + len(BESIDE))
     for s in GROUPS[1]:
         rows[s].start()
+    tell(0)
 
     with scope("slots"):
         peer = (
@@ -198,12 +209,16 @@
             ref[s, 1:2] = jnp.sum(rank, axis=0, keepdims=True) + (EMPTY + over)
     for s in ORDER:
         metas[s].start()
-    with scope("pack_rest"):
-        for group in GROUPS[2:] + GROUPS[:1]:
+    for n, group in enumerate(GROUPS[2:] + GROUPS[:1]):
+        with scope("pack_rest"):
             gather_rows(group)
             for s in group:
                 if s:
                     rows[s].start()
+        if n < len(ROUNDS):
+            hear(n)
+            if n + 1 < len(ROUNDS):
+                tell(n + 1)
 
     others = pl.ds(1, PEERS - 1)
 
@@ -244,15 +259,6 @@
         with scope(f"rows_wait#s={s}"):
             rows[s].wait_recv()
         spread(s)
-    with scope("ranks_wait"):
-        all_ranks.wait_recv()
-    rank_row = own_lanes(ranks_in)
-    rank_col = rank_row.T
-    highest = jnp.zeros((PLANES, SLOTS), jnp.float32)
-    for j in range(PEERS):
-        highest = jnp.maximum(highest, ranks_in[j])
-    flag_ref[0] = jnp.max(jnp.where(highest >= 2 * EMPTY, 1, 0))
-
     best = [jnp.full((1, SLOTS), -1.0, jnp.float32)] * PLANES
     seen = []
 
@@ -283,9 +289,22 @@
                         top = jnp.maximum(top, jnp.where(earlier, part(n, k), -1.0))
                     best[q] = jnp.maximum(best[q], jnp.max(top.T, axis=0, keepdims=True))
 
+    for s in GROUPS[3]:
+        with scope(f"rows_wait#s={s}"):
+            rows[s].wait_recv()
+        spread(s)
+    with scope("ranks_wait"):
+        all_ranks.wait_recv()
+    rank_row = own_lanes(ranks_in)
+    rank_col = rank_row.T
+    highest = jnp.zeros((PLANES, SLOTS), jnp.float32)
+    for j in range(PEERS):
+        highest = jnp.maximum(highest, ranks_in[j])
+    flag_ref[0] = jnp.max(jnp.where(highest >= 2 * EMPTY, 1, 0))
+
     compare(GROUPS[0])
     compare(GROUPS[1])
-    for s in GROUPS[3] + GROUPS[4]:
+    for s in GROUPS[4]:
         with scope(f"rows_wait#s={s}"):
             rows[s].wait_recv()
         spread(s)
@@ -408,6 +427,7 @@
             dma, dma,
             dma((2 * len(FIRST),)), dma,
             dma((PLANES,)), dma((PLANES,)),
+            pltpu.SemaphoreType.REGULAR((len(ROUNDS),)),
         ],
         compiler_params=pltpu.CompilerParams(
             collective_id=number, has_side_effects=True, vmem_limit_bytes=vmem

time: 50.6 us -> 50.1 us (level)
  Pallas kernels: 49.1 us -> 48.5 us
    pallas_call x1, Pallas kernels: 49.1 us -> 48.5 us  [exchange(): pl.pallas_call(functools.partial(kernel, room), out_shape=(jax.ShapeDtype...]
where the time goes in v6:
time: 50.1 us; the launch traced here: 50 us
  Pallas kernels  48.5 us (97%)
  between operations  0.64 us (1%)
  local copies, waits for them, and re-layouts  0.58 us (1%)
    pallas_call x1, Pallas kernels, exchange(): pl.pallas_call(functools.partial(kernel, room), out_shape=(jax.ShapeDtype...  48.5 us

profile of v6, /device:TPU:1, one launch (start us, length us, event | category | flops | bytes accessed | tf_op | source)
XLA Modules:
  0.0 50.0 jit_solution(9640807230451283511)
XLA Ops:
  0.0 48.5 %shard_map.39 = (f32[4,128]{1,0:T(4,128)S(1)}, s32[1]{0:T(128)}) custom-call(bf16[512,768]{1,0:T(8,128)(2,1)} %emb_hbm.1, s32[4,128]{1,0:T(4,128)} %bitcast.2.cid_hbm, s32[4,128]{1,0:T(4,128)} %bitcast.3.rank_hbm), custom_call_target="tpu_custom_call" | custom-call | tf_op jit(solution)/shard_map/pallas_call | solution.py:390
  49.1 0.2 conditional.1
  49.4 0.6 %copy.10 = f32[512]{0:T(512)} copy(f32[512]{0:T(512)S(1)} %get-tuple-element.25) | data formatting | bytes 4096

commit v7 on v6

--- a/solution.py
+++ b/solution.py
@@ -94,25 +94,19 @@
 
 
 def kernel(
-    room, emb_hbm, cid_hbm, rank_hbm, out_ref, flag_ref,
+    room, emb_hbm, cid_hbm, rank_hbm, out_ref, flag_hbm, flag_ref,
     raw, cid_ref, rank_ref, unit, meta_out, meta_in, rows_out, rows_in, dense, arrived, members,
     ranks_out, ranks_in, best_out, best_rows, best_in, far_in, back_out, back_in,
-    raw_sem, meta_sent, meta_landed, rows_sent, rows_landed, dense_sent, dense_landed,
+    raw_sem, cid_sem, rank_sem, meta_sent, meta_landed, rows_sent, rows_landed, dense_sent, dense_landed,
     ranks_sent, ranks_landed, best_sent, best_landed, far_sent, far_landed, back_sent, back_landed, met,
 ):
     here = place()
     z, y, x, c = here
-    load_cid = pltpu.make_async_copy(cid_hbm, cid_ref, raw_sem.at[BLOCKS])
+    load_cid = pltpu.make_async_copy(cid_hbm, cid_ref, cid_sem)
     load_cid.start()
-    loads = [
-        pltpu.make_async_copy(
-            emb_hbm.at[pl.ds(b * 128, 128)], raw.at[pl.ds(b * 128, 128)], raw_sem.at[b]
-        )
-        for b in range(BLOCKS)
-    ]
-    for load in loads:
-        load.start()
-    load_rank = pltpu.make_async_copy(rank_hbm, rank_ref, raw_sem.at[BLOCKS + 1])
+    load = pltpu.make_async_copy(emb_hbm, raw, raw_sem)
+    load.start()
+    load_rank = pltpu.make_async_copy(rank_hbm, rank_ref, rank_sem)
     load_rank.start()
     with scope("greet"):
         barrier = pltpu.get_barrier_semaphore()
@@ -147,18 +141,18 @@
             over = jnp.maximum(over, jnp.where(count < room, 0.0, 2 * EMPTY))
         pack = jnp.concatenate(pack_rows, axis=1)
     with scope("norm"):
+        load.wait()
         for b in range(BLOCKS):
-            loads[b].wait()
             values = raw[b * 128 : (b + 1) * 128].astype(jnp.float32)
             scale = lax.rsqrt(jnp.sum(values * values, axis=1, keepdims=True) + epsilon)
             unit[b * 128 : (b + 1) * 128] = (values * scale).astype(jnp.bfloat16)
 
     rows = {
-        s: send(rows_out.at[s], rows_in.at[s], rows_sent.at[s], rows_landed.at[s], across(here, s))
+        s: send(rows_out.at[s], rows_in.at[s], rows_sent, rows_landed.at[s - 1], across(here, s))
         for s in range(1, PLANES)
     }
     metas = {
-        s: send(meta_out.at[s], meta_in.at[s], meta_sent.at[s], meta_landed.at[s], across(here, s))
+        s: send(meta_out.at[s], meta_in.at[s], meta_sent, meta_landed.at[0 if s in GROUPS[1] else 1], across(here, s))
         for s in range(1, PLANES)
     }
 
@@ -232,23 +226,26 @@
             arrived[s, 0] = placed[:CAP]
         with scope(f"deliver#s={s}"):
             for j in FAR_FIRST:
-                send(dense.at[s, j], arrived.at[s, j], dense_sent.at[s], dense_landed.at[s], within(here, j, 1)).start()
+                send(dense.at[s, j], arrived.at[s, j], dense_sent, dense_landed.at[s], within(here, j, 1)).start()
 
     def all_dense(s):
-        return send(dense.at[s, others], arrived.at[s, others], dense_sent.at[s], dense_landed.at[s], within(here, 1, 1))
+        return send(dense.at[s, others], arrived.at[s, others], dense_sent, dense_landed.at[s], within(here, 1, 1))
 
     all_ranks = send(ranks_in.at[others], ranks_in.at[others], ranks_sent, ranks_landed, within(here, 1, 1))
     all_best = send(best_in.at[others], best_in.at[others], best_sent, best_landed, within(here, 1, 1))
 
     spread(0)
+    def metas_in(n, count):
+        some = meta_in.at[pl.ds(0, count)]
+        return send(some, some, meta_sent, meta_landed.at[n], across(here, 1))
+
+    metas_in(0, len(GROUPS[1])).wait_recv()
     for s in GROUPS[1]:
         with scope(f"rows_wait#s={s}"):
-            metas[s].wait_recv()
             rows[s].wait_recv()
         spread(s)
     with scope("meta_wait"):
-        for s in ORDER[len(GROUPS[1]) :]:
-            metas[s].wait_recv()
+        metas_in(1, PLANES - 1 - len(GROUPS[1])).wait_recv()
     for s in range(PLANES):
         ranks_out[s : s + 1] = meta_in[s, 1:2]
     ranks_in[0] = ranks_out[...]
@@ -301,6 +298,8 @@
     for j in range(PEERS):
         highest = jnp.maximum(highest, ranks_in[j])
     flag_ref[0] = jnp.max(jnp.where(highest >= 2 * EMPTY, 1, 0))
+    save_flag = pltpu.make_async_copy(flag_ref, flag_hbm, cid_sem)
+    save_flag.start()
 
     compare(GROUPS[0])
     compare(GROUPS[1])
@@ -314,9 +313,9 @@
 
     lanes, peers = iota((PEERS, SLOTS), 1), iota((PEERS, SLOTS), 0)
     straight = []
-    for n, (a, b, d, e) in enumerate((*chip, core) for chip in FIRST for core in (1, 0)):
+    for a, b, d, e in [(*chip, core) for chip in FIRST for core in (1, 0)]:
         up, j = lax.rem(z - a + PLANES, PLANES), lax.rem(c + e, 2) * 16 + lax.rem(x - d + 4, 4) * 4 + lax.rem(y - b + 4, 4)
-        straight.append((up, send(best_rows.at[up], far_in.at[up, j], far_sent.at[n], far_landed, device(a, b, d, e))))
+        straight.append((up, send(best_rows.at[up], far_in.at[up, j], far_sent.at[e], far_landed, device(a, b, d, e))))
     with scope("answer"):
         for s in range(PLANES):
             best_rows[s] = best[s]
@@ -331,12 +330,12 @@
         for j in FAR_FIRST:
             send(best_out.at[j], best_in.at[j], best_sent, best_landed, within(here, j, -1)).start()
     best_in[0] = best_out[0]
-    for s in ORDER:
-        metas[s].wait_send()
-        rows[s].wait_send()
-    for s in range(PLANES):
-        all_dense(s).wait_send()
+    metas_in(0, PLANES - 1).wait_send()
+    steps = pl.ds(1, PLANES - 1)
+    send(rows_out.at[steps], rows_out.at[steps], rows_sent, rows_landed.at[0], across(here, 1)).wait_send()
+    send(dense.at[:, others], dense.at[:, others], dense_sent, dense_landed.at[0], across(here, 1)).wait_send()
     all_ranks.wait_send()
+    save_flag.wait()
     with scope("best_wait"):
         all_best.wait_recv()
     with scope("back"):
@@ -349,28 +348,39 @@
                 back_in[0] = line
                 continue
             back_out[s] = line
-            back = send(back_out.at[s], back_in.at[s], back_sent.at[s], back_landed.at[s], across(here, PLANES - s))
+            back = send(back_out.at[s], back_in.at[s], back_sent, back_landed, across(here, PLANES - s))
             wanted = jnp.logical_not(is_first(lax.rem(z + PLANES - s, PLANES), y, x))
             pl.when(wanted)(back.start)
             backs.append((wanted, back))
     all_best.wait_send()
-    for up, copy in straight:
-        pl.when(up != 0)(copy.wait_send)
-    for wanted, back in backs:
-        pl.when(wanted)(back.wait_send)
+    for a in range(PLANES):
+        count = len([chip for chip in FIRST if chip[0] != a])
+
+        @pl.when(z == a)
+        def _():
+            for e in range(2):
+                some = best_in.at[pl.ds(0, count)]
+                send(some, some, far_sent.at[e], far_landed, across(here, 1)).wait_send()
+
+    sent = sum(wanted.astype(jnp.int32) for wanted, _ in backs)
+    for count in range(4, PLANES):
+
+        @pl.when(sent == count)
+        def _():
+            some = back_out.at[pl.ds(0, count)]
+            send(some, some, back_sent, back_landed, across(here, 1)).wait_send()
+
     first = is_first(z, y, x)
 
     @pl.when(jnp.logical_not(first))
     def _():
         with scope("back_wait"):
-            for _, back in backs:
-                back.wait_recv()
+            send(back_in.at[steps], back_in.at[steps], back_sent, back_landed, across(here, 1)).wait_recv()
 
     @pl.when(first)
     def _():
-        steps = far_in.at[pl.ds(1, PLANES - 1)]
         with scope("far_wait"):
-            send(steps, steps, far_sent.at[0], far_landed, across(here, 1)).wait_recv()
+            send(far_in.at[steps], far_in.at[steps], far_sent.at[0], far_landed, across(here, 1)).wait_recv()
         for s in range(1, PLANES):
             tiles = far_in[s].reshape(PEERS, SLOTS)
             back_in[s] = jnp.sum(jnp.where(lanes // CAP == peers, tiles, 0.0), axis=0, keepdims=True)
@@ -398,8 +408,9 @@
             pl.BlockSpec(memory_space=pltpu.HBM),
             pl.BlockSpec(memory_space=pltpu.HBM),
         ],
-        out_specs=(pl.BlockSpec(memory_space=pltpu.VMEM), pl.BlockSpec(memory_space=pltpu.SMEM)),
+        out_specs=(pl.BlockSpec(memory_space=pltpu.VMEM), pl.BlockSpec(memory_space=pltpu.HBM)),
         scratch_shapes=[
+            pltpu.SMEM((1,), jnp.int32),
             pltpu.VMEM((ROWS_DEV, WIDTH), jnp.bfloat16),
             pltpu.VMEM((BLOCKS, 128), jnp.int32),
             pltpu.VMEM((BLOCKS, 128), jnp.int32),
@@ -419,14 +430,14 @@
             pltpu.VMEM((PLANES, PEERS, 1, SLOTS), jnp.float32),
             pltpu.VMEM((PLANES, 1, SLOTS), jnp.float32),
             pltpu.VMEM((PLANES, 1, SLOTS), jnp.float32),
-            dma((BLOCKS + 2,)),
-            dma((PLANES,)), dma((PLANES,)),
-            dma((PLANES,)), dma((PLANES,)),
-            dma((PLANES,)), dma((PLANES,)),
+            dma, dma, dma,
+            dma, dma((2,)),
+            dma, dma((PLANES - 1,)),
+            dma, dma((PLANES,)),
             dma, dma,
             dma, dma,
-            dma((2 * len(FIRST),)), dma,
-            dma((PLANES,)), dma((PLANES,)),
+            dma((2,)), dma,
+            dma, dma,
             pltpu.SemaphoreType.REGULAR((len(ROUNDS),)),
         ],
         compiler_params=pltpu.CompilerParams(

time: 50.1 us -> 48.9 us (0.976)
  Pallas kernels: 48.5 us -> 47.4 us
    pallas_call x1, Pallas kernels: 48.5 us -> 47.4 us  [exchange(): pl.pallas_call(functools.partial(kernel, room), out_shape=(jax.ShapeDtype...]
where the time goes in v7:
time: 48.9 us; the launch traced here: 48.8 us
  Pallas kernels  47.4 us (97%)
  between operations  0.64 us (1%)
  local copies, waits for them, and re-layouts  0.58 us (1%)
    pallas_call x1, Pallas kernels, exchange(): pl.pallas_call(functools.partial(kernel, room), out_shape=(jax.ShapeDtype...  47.4 us

profile of v7, /device:TPU:1, one launch (start us, length us, event | category | flops | bytes accessed | tf_op | source)
XLA Modules:
  0.0 48.8 jit_solution(11889060347026633392)
XLA Ops:
  0.0 47.4 %shard_map.39 = (f32[4,128]{1,0:T(4,128)S(1)}, s32[1]{0:T(128)}) custom-call(bf16[512,768]{1,0:T(8,128)(2,1)} %emb_hbm.1, s32[4,128]{1,0:T(4,128)} %bitcast.2.cid_hbm, s32[4,128]{1,0:T(4,128)} %bitcast.3.rank_hbm), custom_call_target="tpu_custom_call" | custom-call | tf_op jit(solution)/shard_map/pallas_call | solution.py:400
  48.0 0.2 conditional.1
  48.2 0.6 %copy.10 = f32[512]{0:T(512)} copy(f32[512]{0:T(512)S(1)} %get-tuple-element.25) | data formatting | bytes 4096

commit v8 on v7

--- a/solution.py
+++ b/solution.py
@@ -56,6 +56,7 @@
 
 FIRST = [(z, y, x) for z in range(3) for y in range(4) for x in range(4) if z + min(y, 4 - y) + min(x, 4 - x) <= 2]
 BESIDE = (1, 3, 4, 12, 16)
+CLOSE = (1, 7)
 ROUNDS = ((1, 3), (4, 12), (4, 12), (16,))
 FAR_FIRST = sorted(range(1, PEERS), key=lambda j: -hops(j))
 
@@ -95,10 +96,10 @@
 
 def kernel(
     room, emb_hbm, cid_hbm, rank_hbm, out_ref, flag_hbm, flag_ref,
-    raw, cid_ref, rank_ref, unit, meta_out, meta_in, rows_out, rows_in, dense, arrived, members,
+    raw, cid_ref, rank_ref, meta_out, meta_in, rows_out, rows_in, dense, arrived, members,
     ranks_out, ranks_in, best_out, best_rows, best_in, far_in, back_out, back_in,
     raw_sem, cid_sem, rank_sem, meta_sent, meta_landed, rows_sent, rows_landed, dense_sent, dense_landed,
-    ranks_sent, ranks_landed, best_sent, best_landed, far_sent, far_landed, back_sent, back_landed, met,
+    ranks_sent, ranks_landed, best_sent, best_landed, far_sent, far_landed, back_sent, back_landed, linked, met,
 ):
     here = place()
     z, y, x, c = here
@@ -110,7 +111,7 @@
     load_rank.start()
     with scope("greet"):
         barrier = pltpu.get_barrier_semaphore()
-        for s in (4, 3, 5, 2, 6, 1, 7):
+        for s in CLOSE:
             pl.semaphore_signal(barrier, inc=1, device_id=across(here, s), device_id_type=MESH)
         for j in BESIDE:
             pl.semaphore_signal(barrier, inc=1, device_id=within(here, j, 1), device_id_type=MESH)
@@ -122,6 +123,14 @@
     def hear(n):
         with scope(f"hear#n={n}"):
             pl.semaphore_wait(met.at[n], len(ROUNDS[n]))
+
+    def tell_across(n):
+        for s in (1, PLANES - 1):
+            pl.semaphore_signal(linked.at[n], inc=1, device_id=across(here, s), device_id_type=MESH)
+
+    def hear_across(n):
+        with scope(f"hear_across#n={n}"):
+            pl.semaphore_wait(linked.at[n], 2)
 
     with scope("count"):
         load_cid.wait()
@@ -140,19 +149,15 @@
             pack_rows.append(jnp.where(count < room, step[b : b + 1] * SLOTS + count, -1))
             over = jnp.maximum(over, jnp.where(count < room, 0.0, 2 * EMPTY))
         pack = jnp.concatenate(pack_rows, axis=1)
-    with scope("norm"):
+    with scope("load"):
         load.wait()
-        for b in range(BLOCKS):
-            values = raw[b * 128 : (b + 1) * 128].astype(jnp.float32)
-            scale = lax.rsqrt(jnp.sum(values * values, axis=1, keepdims=True) + epsilon)
-            unit[b * 128 : (b + 1) * 128] = (values * scale).astype(jnp.bfloat16)
 
     rows = {
         s: send(rows_out.at[s], rows_in.at[s], rows_sent, rows_landed.at[s - 1], across(here, s))
         for s in range(1, PLANES)
     }
     metas = {
-        s: send(meta_out.at[s], meta_in.at[s], meta_sent, meta_landed.at[0 if s in GROUPS[1] else 1], across(here, s))
+        s: send(meta_out.at[s], meta_in.at[s], meta_sent, meta_landed.at[0 if s in GROUPS[1] else 2 if s in GROUPS[4] else 1], across(here, s))
         for s in range(1, PLANES)
     }
 
@@ -160,7 +165,9 @@
         chosen = jnp.concatenate(
             [jnp.where(pack == s * SLOTS + iota((room, ROWS_DEV), 0), 1.0, 0.0) for s in group], axis=0
         ).astype(jnp.bfloat16)
-        packed = jnp.dot(chosen, unit[...], preferred_element_type=jnp.float32).astype(jnp.bfloat16)
+        picked = jnp.dot(chosen, raw[...], preferred_element_type=jnp.float32)
+        scale = lax.rsqrt(jnp.sum(picked * picked, axis=1, keepdims=True) + epsilon)
+        packed = (picked * scale).astype(jnp.bfloat16)
         for n, s in enumerate(group):
             ref = rows_in if s == 0 else rows_out
             ref[s] = packed[n * room : (n + 1) * room]
@@ -168,9 +175,12 @@
     with scope("pack"):
         gather_rows(GROUPS[1])
     with scope("barrier_wait"):
-        pl.semaphore_wait(barrier, PLANES - 1 + len(BESIDE))
+        pl.semaphore_wait(barrier, len(CLOSE) + len(BESIDE))
+    pl.when(z == 1)(lambda: pl.delay(800))
+    pl.when(z == 2)(lambda: pl.delay(1200))
     for s in GROUPS[1]:
         rows[s].start()
+    tell_across(0)
     tell(0)
 
     with scope("slots"):
@@ -185,6 +195,11 @@
                 same += jnp.where(alike & before if a == b else alike, 1.0, 0.0)
             position = jnp.sum(same, axis=0, keepdims=True).astype(jnp.int32)
             slot_rows.append(step[b : b + 1] * SLOTS + peer[b : b + 1] * CAP + position)
+    hear_across(0)
+    tell_across(1)
+    hear(0)
+    tell(1)
+    with scope("names"):
         over = jnp.max(over, axis=1, keepdims=True)
         slot_turned = jnp.concatenate(slot_rows + pack_rows, axis=0).T
         load_rank.wait()
@@ -201,18 +216,26 @@
             ref = meta_in if s == 0 else meta_out
             ref[s, 0:1] = jnp.sum(name, axis=0, keepdims=True) - 1.0
             ref[s, 1:2] = jnp.sum(rank, axis=0, keepdims=True) + (EMPTY + over)
-    for s in ORDER:
+    with scope("pack_rest"):
+        gather_rows(GROUPS[2])
+    hear_across(1)
+    tell_across(2)
+    for s in GROUPS[1] + GROUPS[2] + GROUPS[3]:
         metas[s].start()
-    for n, group in enumerate(GROUPS[2:] + GROUPS[:1]):
-        with scope("pack_rest"):
-            gather_rows(group)
-            for s in group:
-                if s:
-                    rows[s].start()
-        if n < len(ROUNDS):
-            hear(n)
-            if n + 1 < len(ROUNDS):
-                tell(n + 1)
+    for s in GROUPS[2]:
+        rows[s].start()
+    hear(1)
+    tell(2)
+    with scope("pack_rest"):
+        gather_rows(GROUPS[3])
+    with scope("pack_rest"):
+        gather_rows(GROUPS[4] + GROUPS[0])
+    hear_across(2)
+    for s in GROUPS[4]:
+        metas[s].start()
+    hear(2)
+    tell(3)
+    hear(3)
 
     others = pl.ds(1, PEERS - 1)
 
@@ -243,19 +266,25 @@
     for s in GROUPS[1]:
         with scope(f"rows_wait#s={s}"):
             rows[s].wait_recv()
+    for s in GROUPS[3]:
+        rows[s].start()
+    for s in GROUPS[1]:
         spread(s)
     with scope("meta_wait"):
-        metas_in(1, PLANES - 1 - len(GROUPS[1])).wait_recv()
+        metas_in(1, len(GROUPS[2] + GROUPS[3])).wait_recv()
+    for s in GROUPS[2]:
+        with scope(f"rows_wait#s={s}"):
+            rows[s].wait_recv()
+        spread(s)
+    for s in GROUPS[4]:
+        rows[s].start()
+    metas_in(2, len(GROUPS[4])).wait_recv()
     for s in range(PLANES):
         ranks_out[s : s + 1] = meta_in[s, 1:2]
     ranks_in[0] = ranks_out[...]
     for j in FAR_FIRST:
         send(ranks_out, ranks_in.at[j], ranks_sent, ranks_landed, within(here, j, 1)).start()
 
-    for s in GROUPS[2]:
-        with scope(f"rows_wait#s={s}"):
-            rows[s].wait_recv()
-        spread(s)
     best = [jnp.full((1, SLOTS), -1.0, jnp.float32)] * PLANES
     seen = []
 
@@ -290,6 +319,10 @@
         with scope(f"rows_wait#s={s}"):
             rows[s].wait_recv()
         spread(s)
+    for s in GROUPS[4]:
+        with scope(f"rows_wait#s={s}"):
+            rows[s].wait_recv()
+        spread(s)
     with scope("ranks_wait"):
         all_ranks.wait_recv()
     rank_row = own_lanes(ranks_in)
@@ -303,10 +336,6 @@
 
     compare(GROUPS[0])
     compare(GROUPS[1])
-    for s in GROUPS[4]:
-        with scope(f"rows_wait#s={s}"):
-            rows[s].wait_recv()
-        spread(s)
     compare(GROUPS[2])
     for s in GROUPS[3] + GROUPS[4]:
         compare((s,))
@@ -414,7 +443,6 @@
             pltpu.VMEM((ROWS_DEV, WIDTH), jnp.bfloat16),
             pltpu.VMEM((BLOCKS, 128), jnp.int32),
             pltpu.VMEM((BLOCKS, 128), jnp.int32),
-            pltpu.VMEM((ROWS_DEV, WIDTH), jnp.bfloat16),
             pltpu.VMEM((PLANES, 2, SLOTS), jnp.float32),
             pltpu.VMEM((PLANES, 2, SLOTS), jnp.float32),
             pltpu.VMEM((PLANES, room, WIDTH), jnp.bfloat16),
@@ -431,13 +459,14 @@
             pltpu.VMEM((PLANES, 1, SLOTS), jnp.float32),
             pltpu.VMEM((PLANES, 1, SLOTS), jnp.float32),
             dma, dma, dma,
-            dma, dma((2,)),
+            dma, dma((3,)),
             dma, dma((PLANES - 1,)),
             dma, dma((PLANES,)),
             dma, dma,
             dma, dma,
             dma((2,)), dma,
             dma, dma,
+            pltpu.SemaphoreType.REGULAR((3,)),
             pltpu.SemaphoreType.REGULAR((len(ROUNDS),)),
         ],
         compiler_params=pltpu.CompilerParams(

time: 48.9 us -> 47.6 us (0.973)
  Pallas kernels: 47.4 us -> 46.1 us
    pallas_call x1, Pallas kernels: 47.4 us -> 46.1 us  [exchange(): pl.pallas_call(functools.partial(kernel, room), out_shape=(jax.ShapeDtype...]
where the time goes in v8:
time: 47.6 us; the launch traced here: 47.5 us
  Pallas kernels  46.1 us (97%)
  between operations  0.64 us (1%)
  local copies, waits for them, and re-layouts  0.58 us (1%)
    pallas_call x1, Pallas kernels, exchange(): pl.pallas_call(functools.partial(kernel, room), out_shape=(jax.ShapeDtype...  46.1 us

profile of v8, /device:TPU:1, one launch (start us, length us, event | category | flops | bytes accessed | tf_op | source)
XLA Modules:
  0.0 47.5 jit_solution(3279419386635191800)
XLA Ops:
  0.0 46.1 %shard_map.39 = (f32[4,128]{1,0:T(4,128)S(1)}, s32[1]{0:T(128)}) custom-call(bf16[512,768]{1,0:T(8,128)(2,1)} %emb_hbm.1, s32[4,128]{1,0:T(4,128)} %bitcast.2.cid_hbm, s32[4,128]{1,0:T(4,128)} %bitcast.3.rank_hbm), custom_call_target="tpu_custom_call" | custom-call | tf_op jit(solution)/shard_map/pallas_call | solution.py:429
  46.7 0.2 conditional.1
  47.0 0.6 %copy.10 = f32[512]{0:T(512)} copy(f32[512]{0:T(512)S(1)} %get-tuple-element.25) | data formatting | bytes 4096

commit v9 on v8

--- a/solution.py
+++ b/solution.py
@@ -21,6 +21,8 @@
 EMPTY = float(1 << 17)
 GROUPS = ((0,), (1, 7), (2, 6), (5, 3), (4,))
 ORDER = sum(GROUPS[1:], ())
+TOGETHER = (GROUPS[0] + GROUPS[1], GROUPS[2]) + tuple((s,) for s in GROUPS[3] + GROUPS[4])
+SHARED = {s: n for n, steps in enumerate(TOGETHER) for s in steps}
 epsilon = 1e-06
 
 
@@ -98,8 +100,8 @@
     room, emb_hbm, cid_hbm, rank_hbm, out_ref, flag_hbm, flag_ref,
     raw, cid_ref, rank_ref, meta_out, meta_in, rows_out, rows_in, dense, arrived, members,
     ranks_out, ranks_in, best_out, best_rows, best_in, far_in, back_out, back_in,
-    raw_sem, cid_sem, rank_sem, meta_sent, meta_landed, rows_sent, rows_landed, dense_sent, dense_landed,
-    ranks_sent, ranks_landed, best_sent, best_landed, far_sent, far_landed, back_sent, back_landed, linked, met,
+    raw_sem, cid_sem, meta_landed, rows_sent, rows_landed, dense_sent, dense_landed,
+    small_sent, ranks_landed, far_sent, far_landed, best_landed, back_landed, linked, met,
 ):
     here = place()
     z, y, x, c = here
@@ -107,8 +109,6 @@
     load_cid.start()
     load = pltpu.make_async_copy(emb_hbm, raw, raw_sem)
     load.start()
-    load_rank = pltpu.make_async_copy(rank_hbm, rank_ref, rank_sem)
-    load_rank.start()
     with scope("greet"):
         barrier = pltpu.get_barrier_semaphore()
         for s in CLOSE:
@@ -118,19 +118,19 @@
 
     def tell(n):
         for j in ROUNDS[n]:
-            pl.semaphore_signal(met.at[n], inc=1, device_id=within(here, j, 1), device_id_type=MESH)
+            pl.semaphore_signal(met.at[(0, 1, 0, 2)[n]], inc=1, device_id=within(here, j, 1), device_id_type=MESH)
 
     def hear(n):
         with scope(f"hear#n={n}"):
-            pl.semaphore_wait(met.at[n], len(ROUNDS[n]))
+            pl.semaphore_wait(met.at[(0, 1, 0, 2)[n]], len(ROUNDS[n]))
 
     def tell_across(n):
         for s in (1, PLANES - 1):
-            pl.semaphore_signal(linked.at[n], inc=1, device_id=across(here, s), device_id_type=MESH)
+            pl.semaphore_signal(linked.at[n % 2], inc=1, device_id=across(here, s), device_id_type=MESH)
 
     def hear_across(n):
         with scope(f"hear_across#n={n}"):
-            pl.semaphore_wait(linked.at[n], 2)
+            pl.semaphore_wait(linked.at[n % 2], 2)
 
     with scope("count"):
         load_cid.wait()
@@ -149,15 +149,17 @@
             pack_rows.append(jnp.where(count < room, step[b : b + 1] * SLOTS + count, -1))
             over = jnp.maximum(over, jnp.where(count < room, 0.0, 2 * EMPTY))
         pack = jnp.concatenate(pack_rows, axis=1)
+    load_rank = pltpu.make_async_copy(rank_hbm, rank_ref, cid_sem)
+    load_rank.start()
     with scope("load"):
         load.wait()
 
     rows = {
-        s: send(rows_out.at[s], rows_in.at[s], rows_sent, rows_landed.at[s - 1], across(here, s))
+        s: send(rows_out.at[s], rows_in.at[s], rows_sent, rows_landed.at[0 if s in GROUPS[1] else ORDER.index(s) - 1], across(here, s))
         for s in range(1, PLANES)
     }
     metas = {
-        s: send(meta_out.at[s], meta_in.at[s], meta_sent, meta_landed.at[0 if s in GROUPS[1] else 2 if s in GROUPS[4] else 1], across(here, s))
+        s: send(meta_out.at[s], meta_in.at[s], small_sent, meta_landed.at[0 if s in GROUPS[1] else 2 if s in GROUPS[4] else 1], across(here, s))
         for s in range(1, PLANES)
     }
 
@@ -233,6 +235,11 @@
     hear_across(2)
     for s in GROUPS[4]:
         metas[s].start()
+    with scope("rows_wait#s=1"):
+        first_two = rows_in.at[pl.ds(0, len(GROUPS[1]))]
+        send(first_two, first_two, rows_sent, rows_landed.at[0], across(here, 1)).wait_recv()
+    for s in GROUPS[3]:
+        rows[s].start()
     hear(2)
     tell(3)
     hear(3)
@@ -249,25 +256,21 @@
             arrived[s, 0] = placed[:CAP]
         with scope(f"deliver#s={s}"):
             for j in FAR_FIRST:
-                send(dense.at[s, j], arrived.at[s, j], dense_sent, dense_landed.at[s], within(here, j, 1)).start()
-
-    def all_dense(s):
-        return send(dense.at[s, others], arrived.at[s, others], dense_sent, dense_landed.at[s], within(here, 1, 1))
-
-    all_ranks = send(ranks_in.at[others], ranks_in.at[others], ranks_sent, ranks_landed, within(here, 1, 1))
-    all_best = send(best_in.at[others], best_in.at[others], best_sent, best_landed, within(here, 1, 1))
+                send(dense.at[s, j], arrived.at[s, j], dense_sent, dense_landed.at[SHARED[s]], within(here, j, 1)).start()
+
+    def all_dense(n):
+        some = arrived.at[pl.ds(0, len(TOGETHER[n])), others]
+        return send(some, some, dense_sent, dense_landed.at[n], within(here, 1, 1))
+
+    all_ranks = send(ranks_in.at[others], ranks_in.at[others], small_sent, ranks_landed, within(here, 1, 1))
+    all_best = send(best_in.at[others], best_in.at[others], small_sent, best_landed, within(here, 1, 1))
 
     spread(0)
     def metas_in(n, count):
         some = meta_in.at[pl.ds(0, count)]
-        return send(some, some, meta_sent, meta_landed.at[n], across(here, 1))
+        return send(some, some, small_sent, meta_landed.at[n], across(here, 1))
 
     metas_in(0, len(GROUPS[1])).wait_recv()
-    for s in GROUPS[1]:
-        with scope(f"rows_wait#s={s}"):
-            rows[s].wait_recv()
-    for s in GROUPS[3]:
-        rows[s].start()
     for s in GROUPS[1]:
         spread(s)
     with scope("meta_wait"):
@@ -279,11 +282,12 @@
     for s in GROUPS[4]:
         rows[s].start()
     metas_in(2, len(GROUPS[4])).wait_recv()
+    metas_in(0, PLANES - 1).wait_send()
     for s in range(PLANES):
         ranks_out[s : s + 1] = meta_in[s, 1:2]
     ranks_in[0] = ranks_out[...]
     for j in FAR_FIRST:
-        send(ranks_out, ranks_in.at[j], ranks_sent, ranks_landed, within(here, j, 1)).start()
+        send(ranks_out, ranks_in.at[j], small_sent, ranks_landed, within(here, j, 1)).start()
 
     best = [jnp.full((1, SLOTS), -1.0, jnp.float32)] * PLANES
     seen = []
@@ -291,8 +295,9 @@
     def compare(group):
         known = len(seen)
         for s in group:
-            with scope(f"dense_wait#s={s}"):
-                all_dense(s).wait_recv()
+            if s == TOGETHER[SHARED[s]][0]:
+                with scope(f"dense_wait#s={s}"):
+                    all_dense(SHARED[s]).wait_recv()
             members[len(seen) * SLOTS : (len(seen) + 1) * SLOTS] = arrived[s].reshape(SLOTS, WIDTH)
             seen.append(s)
         with scope(f"scores#n={len(seen)}"):
@@ -340,6 +345,8 @@
     for s in GROUPS[3] + GROUPS[4]:
         compare((s,))
 
+    all_ranks.wait_send()
+
     lanes, peers = iota((PEERS, SLOTS), 1), iota((PEERS, SLOTS), 0)
     straight = []
     for a, b, d, e in [(*chip, core) for chip in FIRST for core in (1, 0)]:
@@ -357,17 +364,16 @@
             answers = jnp.where(lanes // CAP == s, picked, answers)
         best_out[...] = answers.reshape(PEERS, 1, SLOTS)
         for j in FAR_FIRST:
-            send(best_out.at[j], best_in.at[j], best_sent, best_landed, within(here, j, -1)).start()
+            send(best_out.at[j], best_in.at[j], small_sent, best_landed, within(here, j, -1)).start()
     best_in[0] = best_out[0]
-    metas_in(0, PLANES - 1).wait_send()
     steps = pl.ds(1, PLANES - 1)
     send(rows_out.at[steps], rows_out.at[steps], rows_sent, rows_landed.at[0], across(here, 1)).wait_send()
     send(dense.at[:, others], dense.at[:, others], dense_sent, dense_landed.at[0], across(here, 1)).wait_send()
-    all_ranks.wait_send()
     save_flag.wait()
     with scope("best_wait"):
         all_best.wait_recv()
     with scope("back"):
+        all_best.wait_send()
         answers = best_in[...].reshape(PEERS, SLOTS)
         backs = []
         for s in (4, 3, 5, 2, 6, 1, 7, 0):
@@ -377,11 +383,10 @@
                 back_in[0] = line
                 continue
             back_out[s] = line
-            back = send(back_out.at[s], back_in.at[s], back_sent, back_landed, across(here, PLANES - s))
+            back = send(back_out.at[s], back_in.at[s], small_sent, back_landed, across(here, PLANES - s))
             wanted = jnp.logical_not(is_first(lax.rem(z + PLANES - s, PLANES), y, x))
             pl.when(wanted)(back.start)
             backs.append((wanted, back))
-    all_best.wait_send()
     for a in range(PLANES):
         count = len([chip for chip in FIRST if chip[0] != a])
 
@@ -397,14 +402,14 @@
         @pl.when(sent == count)
         def _():
             some = back_out.at[pl.ds(0, count)]
-            send(some, some, back_sent, back_landed, across(here, 1)).wait_send()
+            send(some, some, small_sent, back_landed, across(here, 1)).wait_send()
 
     first = is_first(z, y, x)
 
     @pl.when(jnp.logical_not(first))
     def _():
         with scope("back_wait"):
-            send(back_in.at[steps], back_in.at[steps], back_sent, back_landed, across(here, 1)).wait_recv()
+            send(back_in.at[steps], back_in.at[steps], small_sent, back_landed, across(here, 1)).wait_recv()
 
     @pl.when(first)
     def _():
@@ -458,16 +463,15 @@
             pltpu.VMEM((PLANES, PEERS, 1, SLOTS), jnp.float32),
             pltpu.VMEM((PLANES, 1, SLOTS), jnp.float32),
             pltpu.VMEM((PLANES, 1, SLOTS), jnp.float32),
-            dma, dma, dma,
-            dma, dma((3,)),
-            dma, dma((PLANES - 1,)),
-            dma, dma((PLANES,)),
             dma, dma,
+            dma((3,)),
+            dma, dma((PLANES - 2,)),
+            dma, dma((len(TOGETHER),)),
             dma, dma,
             dma((2,)), dma,
             dma, dma,
+            pltpu.SemaphoreType.REGULAR((2,)),
             pltpu.SemaphoreType.REGULAR((3,)),
-            pltpu.SemaphoreType.REGULAR((len(ROUNDS),)),
         ],
         compiler_params=pltpu.CompilerParams(
             collective_id=number, has_side_effects=True, vmem_limit_bytes=vmem

time: 47.6 us -> 47.4 us (level)
  no operation moved by 1% of the time
where the time goes in v9:
time: 47.4 us; the launch traced here: 47.3 us
  Pallas kernels  45.9 us (97%)
  between operations  0.64 us (1%)
  local copies, waits for them, and re-layouts  0.58 us (1%)
    pallas_call x1, Pallas kernels, exchange(): pl.pallas_call(functools.partial(kernel, room), out_shape=(jax.ShapeDtype...  45.9 us

profile of v9, /device:TPU:1, one launch (start us, length us, event | category | flops | bytes accessed | tf_op | source)
XLA Modules:
  0.0 47.3 jit_solution(14174746231822703654)
XLA Ops:
  0.0 45.9 %shard_map.39 = (f32[4,128]{1,0:T(4,128)S(1)}, s32[1]{0:T(128)}) custom-call(bf16[512,768]{1,0:T(8,128)(2,1)} %emb_hbm.1, s32[4,128]{1,0:T(4,128)} %bitcast.2.cid_hbm, s32[4,128]{1,0:T(4,128)} %bitcast.3.rank_hbm), custom_call_target="tpu_custom_call" | custom-call | tf_op jit(solution)/shard_map/pallas_call | solution.py:434
  46.5 0.2 conditional.1
  46.7 0.6 %copy.10 = f32[512]{0:T(512)} copy(f32[512]{0:T(512)S(1)} %get-tuple-element.25) | data formatting | bytes 4096

commit v10 on v9

--- a/solution.py
+++ b/solution.py
@@ -238,6 +238,8 @@
     with scope("rows_wait#s=1"):
         first_two = rows_in.at[pl.ds(0, len(GROUPS[1]))]
         send(first_two, first_two, rows_sent, rows_landed.at[0], across(here, 1)).wait_recv()
+    tell_across(3)
+    hear_across(3)
     for s in GROUPS[3]:
         rows[s].start()
     hear(2)
@@ -278,9 +280,10 @@
     for s in GROUPS[2]:
         with scope(f"rows_wait#s={s}"):
             rows[s].wait_recv()
+        if s == GROUPS[2][0]:
+            for far in GROUPS[4]:
+                rows[far].start()
         spread(s)
-    for s in GROUPS[4]:
-        rows[s].start()
     metas_in(2, len(GROUPS[4])).wait_recv()
     metas_in(0, PLANES - 1).wait_send()
     for s in range(PLANES):

time: 47.4 us -> 47.3 us (level)
  no operation moved by 1% of the time
where the time goes in v10:
time: 47.3 us; the launch traced here: 47.2 us
  Pallas kernels  45.8 us (97%)
  between operations  0.64 us (1%)
  local copies, waits for them, and re-layouts  0.58 us (1%)
    pallas_call x1, Pallas kernels, exchange(): pl.pallas_call(functools.partial(kernel, room), out_shape=(jax.ShapeDtype...  45.8 us

profile of v10, /device:TPU:1, one launch (start us, length us, event | category | flops | bytes accessed | tf_op | source)
XLA Modules:
  0.0 47.2 jit_solution(5409382938126860043)
XLA Ops:
  0.0 45.8 %shard_map.39 = (f32[4,128]{1,0:T(4,128)S(1)}, s32[1]{0:T(128)}) custom-call(bf16[512,768]{1,0:T(8,128)(2,1)} %emb_hbm.1, s32[4,128]{1,0:T(4,128)} %bitcast.2.cid_hbm, s32[4,128]{1,0:T(4,128)} %bitcast.3.rank_hbm), custom_call_target="tpu_custom_call" | custom-call | tf_op jit(solution)/shard_map/pallas_call | solution.py:437
  46.4 0.2 conditional.1
  46.6 0.6 %copy.10 = f32[512]{0:T(512)} copy(f32[512]{0:T(512)S(1)} %get-tuple-element.25) | data formatting | bytes 4096

commit v11 on v10

--- a/solution.py
+++ b/solution.py
@@ -178,8 +178,6 @@
         gather_rows(GROUPS[1])
     with scope("barrier_wait"):
         pl.semaphore_wait(barrier, len(CLOSE) + len(BESIDE))
-    pl.when(z == 1)(lambda: pl.delay(800))
-    pl.when(z == 2)(lambda: pl.delay(1200))
     for s in GROUPS[1]:
         rows[s].start()
     tell_across(0)
@@ -197,35 +195,42 @@
                 same += jnp.where(alike & before if a == b else alike, 1.0, 0.0)
             position = jnp.sum(same, axis=0, keepdims=True).astype(jnp.int32)
             slot_rows.append(step[b : b + 1] * SLOTS + peer[b : b + 1] * CAP + position)
+    over = jnp.max(over, axis=1, keepdims=True)
+    slot_turned = jnp.concatenate(slot_rows + pack_rows, axis=0).T
+    load_rank.wait()
+    rank_turned = (rank_ref[...].astype(jnp.float32) - EMPTY).T
+    lane = iota((128, 128), 1)
+
+    def write_names(group):
+        with scope("names"):
+            for s in group:
+                name = jnp.zeros((128, 128), jnp.float32)
+                rank = jnp.zeros((128, 128), jnp.float32)
+                for b in range(BLOCKS):
+                    slots = slot_turned[:, b : b + 1]
+                    packs = slot_turned[:, BLOCKS + b : BLOCKS + b + 1]
+                    name = jnp.where(packs == s * SLOTS + lane, (slots - (s * SLOTS - 1)).astype(jnp.float32), name)
+                    rank = jnp.where(slots == s * SLOTS + lane, rank_turned[:, b : b + 1], rank)
+                ref = meta_in if s == 0 else meta_out
+                ref[s, 0:1] = jnp.sum(name, axis=0, keepdims=True) - 1.0
+                ref[s, 1:2] = jnp.sum(rank, axis=0, keepdims=True) + (EMPTY + over)
+
     hear_across(0)
     tell_across(1)
-    hear(0)
-    tell(1)
-    with scope("names"):
-        over = jnp.max(over, axis=1, keepdims=True)
-        slot_turned = jnp.concatenate(slot_rows + pack_rows, axis=0).T
-        load_rank.wait()
-        rank_turned = (rank_ref[...].astype(jnp.float32) - EMPTY).T
-        lane = iota((128, 128), 1)
-        for s in range(PLANES):
-            name = jnp.zeros((128, 128), jnp.float32)
-            rank = jnp.zeros((128, 128), jnp.float32)
-            for b in range(BLOCKS):
-                slots = slot_turned[:, b : b + 1]
-                packs = slot_turned[:, BLOCKS + b : BLOCKS + b + 1]
-                name = jnp.where(packs == s * SLOTS + lane, (slots - (s * SLOTS - 1)).astype(jnp.float32), name)
-                rank = jnp.where(slots == s * SLOTS + lane, rank_turned[:, b : b + 1], rank)
-            ref = meta_in if s == 0 else meta_out
-            ref[s, 0:1] = jnp.sum(name, axis=0, keepdims=True) - 1.0
-            ref[s, 1:2] = jnp.sum(rank, axis=0, keepdims=True) + (EMPTY + over)
+    write_names(GROUPS[1])
+    for s in GROUPS[1]:
+        metas[s].start()
     with scope("pack_rest"):
         gather_rows(GROUPS[2])
     hear_across(1)
     tell_across(2)
-    for s in GROUPS[1] + GROUPS[2] + GROUPS[3]:
-        metas[s].start()
     for s in GROUPS[2]:
         rows[s].start()
+    hear(0)
+    tell(1)
+    write_names(GROUPS[2] + GROUPS[3] + GROUPS[4] + GROUPS[0])
+    for s in GROUPS[2] + GROUPS[3]:
+        metas[s].start()
     hear(1)
     tell(2)
     with scope("pack_rest"):
@@ -238,8 +243,6 @@
     with scope("rows_wait#s=1"):
         first_two = rows_in.at[pl.ds(0, len(GROUPS[1]))]
         send(first_two, first_two, rows_sent, rows_landed.at[0], across(here, 1)).wait_recv()
-    tell_across(3)
-    hear_across(3)
     for s in GROUPS[3]:
         rows[s].start()
     hear(2)

time: 47.3 us -> 47.3 us (level)
  no operation moved by 1% of the time
where the time goes in v11:
time: 47.3 us; the launch traced here: 47.2 us
  Pallas kernels  45.7 us (97%)
  between operations  0.64 us (1%)
  local copies, waits for them, and re-layouts  0.58 us (1%)
    pallas_call x1, Pallas kernels, exchange(): pl.pallas_call(functools.partial(kernel, room), out_shape=(jax.ShapeDtype...  45.7 us

profile of v11, /device:TPU:1, one launch (start us, length us, event | category | flops | bytes accessed | tf_op | source)
XLA Modules:
  0.0 47.2 jit_solution(15493617298138642276)
XLA Ops:
  0.0 45.7 %shard_map.39 = (f32[4,128]{1,0:T(4,128)S(1)}, s32[1]{0:T(128)}) custom-call(bf16[512,768]{1,0:T(8,128)(2,1)} %emb_hbm.1, s32[4,128]{1,0:T(4,128)} %bitcast.2.cid_hbm, s32[4,128]{1,0:T(4,128)} %bitcast.3.rank_hbm), custom_call_target="tpu_custom_call" | custom-call | tf_op jit(solution)/shard_map/pallas_call | solution.py:440
  46.4 0.2 conditional.1
  46.6 0.6 %copy.10 = f32[512]{0:T(512)} copy(f32[512]{0:T(512)S(1)} %get-tuple-element.25) | data formatting | bytes 4096

commit v12 on v11

--- a/solution.py
+++ b/solution.py
@@ -280,12 +280,11 @@
         spread(s)
     with scope("meta_wait"):
         metas_in(1, len(GROUPS[2] + GROUPS[3])).wait_recv()
+    for s in GROUPS[4]:
+        rows[s].start()
     for s in GROUPS[2]:
         with scope(f"rows_wait#s={s}"):
             rows[s].wait_recv()
-        if s == GROUPS[2][0]:
-            for far in GROUPS[4]:
-                rows[far].start()
         spread(s)
     metas_in(2, len(GROUPS[4])).wait_recv()
     metas_in(0, PLANES - 1).wait_send()
@@ -312,19 +311,18 @@
             def part(n, k):
                 return scores[n * SLOTS : (n + 1) * SLOTS, k * SLOTS : (k + 1) * SLOTS]
 
+            over_old = [jnp.full((SLOTS, SLOTS), -1.0, jnp.float32) for _ in group]
             for k, q in enumerate(seen):
                 top = jnp.full((SLOTS, SLOTS), -1.0, jnp.float32)
                 for n, m in enumerate(group):
                     earlier = rank_col[:, m : m + 1] < rank_row[q : q + 1]
                     top = jnp.maximum(top, jnp.where(earlier, part(n, k), -1.0))
+                    if k < known:
+                        over_old[n] = jnp.maximum(over_old[n], jnp.where(earlier, -1.0, part(n, k)))
                 best[q] = jnp.maximum(best[q], jnp.max(top, axis=0, keepdims=True))
             for n, q in enumerate(group):
                 if known:
-                    top = jnp.full((SLOTS, SLOTS), -1.0, jnp.float32)
-                    for k, m in enumerate(seen[:known]):
-                        earlier = rank_row[m : m + 1] < rank_col[:, q : q + 1]
-                        top = jnp.maximum(top, jnp.where(earlier, part(n, k), -1.0))
-                    best[q] = jnp.maximum(best[q], jnp.max(top.T, axis=0, keepdims=True))
+                    best[q] = jnp.maximum(best[q], jnp.max(over_old[n].T, axis=0, keepdims=True))
 
     for s in GROUPS[3]:
         with scope(f"rows_wait#s={s}"):

time: 47.3 us -> 47.3 us (level)
  no operation moved by 1% of the time
where the time goes in v12:
time: 47.3 us; the launch traced here: 47.2 us
  Pallas kernels  45.7 us (97%)
  between operations  0.64 us (1%)
  local copies, waits for them, and re-layouts  0.58 us (1%)
    pallas_call x1, Pallas kernels, exchange(): pl.pallas_call(functools.partial(kernel, room), out_shape=(jax.ShapeDtype...  45.7 us

profile of v12, /device:TPU:1, one launch (start us, length us, event | category | flops | bytes accessed | tf_op | source)
XLA Modules:
  0.0 47.2 jit_solution(8325017954031090664)
XLA Ops:
  0.0 45.7 %shard_map.39 = (f32[4,128]{1,0:T(4,128)S(1)}, s32[1]{0:T(128)}) custom-call(bf16[512,768]{1,0:T(8,128)(2,1)} %emb_hbm.1, s32[4,128]{1,0:T(4,128)} %bitcast.2.cid_hbm, s32[4,128]{1,0:T(4,128)} %bitcast.3.rank_hbm), custom_call_target="tpu_custom_call" | custom-call | tf_op jit(solution)/shard_map/pallas_call | solution.py:438
  46.3 0.2 conditional.1
  46.6 0.6 %copy.10 = f32[512]{0:T(512)} copy(f32[512]{0:T(512)S(1)} %get-tuple-element.25) | data formatting | bytes 4096

commit v13 on v12

--- a/solution.py
+++ b/solution.py
@@ -56,15 +56,22 @@
     return min(j % 4, 4 - j % 4) + min(j // 4 % 4, 4 - j // 4 % 4)
 
 
-FIRST = [(z, y, x) for z in range(3) for y in range(4) for x in range(4) if z + min(y, 4 - y) + min(x, 4 - x) <= 2]
+FIRST = [
+    (z, y, x, c)
+    for z in range(4)
+    for y in range(4)
+    for x in range(4)
+    for c in (1, 0)
+    if z + min(y, 4 - y) + min(x, 4 - x) + c <= 3
+]
 BESIDE = (1, 3, 4, 12, 16)
 CLOSE = (1, 7)
 ROUNDS = ((1, 3), (4, 12), (4, 12), (16,))
 FAR_FIRST = sorted(range(1, PEERS), key=lambda j: -hops(j))
 
 
-def is_first(z, y, x):
-    return z + jnp.minimum(y, 4 - y) + jnp.minimum(x, 4 - x) <= 2
+def is_first(z, y, x, c):
+    return z + jnp.minimum(y, 4 - y) + jnp.minimum(x, 4 - x) + c <= 3
 
 
 def send(src, dst, sent, landed, to):
@@ -353,7 +360,7 @@
 
     lanes, peers = iota((PEERS, SLOTS), 1), iota((PEERS, SLOTS), 0)
     straight = []
-    for a, b, d, e in [(*chip, core) for chip in FIRST for core in (1, 0)]:
+    for a, b, d, e in FIRST:
         up, j = lax.rem(z - a + PLANES, PLANES), lax.rem(c + e, 2) * 16 + lax.rem(x - d + 4, 4) * 4 + lax.rem(y - b + 4, 4)
         straight.append((up, send(best_rows.at[up], far_in.at[up, j], far_sent.at[e], far_landed, device(a, b, d, e))))
     with scope("answer"):
@@ -388,27 +395,27 @@
                 continue
             back_out[s] = line
             back = send(back_out.at[s], back_in.at[s], small_sent, back_landed, across(here, PLANES - s))
-            wanted = jnp.logical_not(is_first(lax.rem(z + PLANES - s, PLANES), y, x))
+            wanted = jnp.logical_not(is_first(lax.rem(z + PLANES - s, PLANES), y, x, c))
             pl.when(wanted)(back.start)
             backs.append((wanted, back))
     for a in range(PLANES):
-        count = len([chip for chip in FIRST if chip[0] != a])
+        counts = [len([to for to in FIRST if to[0] != a and to[3] == e]) for e in range(2)]
 
         @pl.when(z == a)
         def _():
-            for e in range(2):
+            for e, count in enumerate(counts):
                 some = best_in.at[pl.ds(0, count)]
                 send(some, some, far_sent.at[e], far_landed, across(here, 1)).wait_send()
 
     sent = sum(wanted.astype(jnp.int32) for wanted, _ in backs)
-    for count in range(4, PLANES):
+    for count in range(3, PLANES):
 
         @pl.when(sent == count)
         def _():
             some = back_out.at[pl.ds(0, count)]
             send(some, some, small_sent, back_landed, across(here, 1)).wait_send()
 
-    first = is_first(z, y, x)
+    first = is_first(z, y, x, c)
 
     @pl.when(jnp.logical_not(first))
     def _():

time: 47.3 us -> 47.3 us (level)
  no operation moved by 1% of the time
where the time goes in v13:
time: 47.3 us; the launch traced here: 47.2 us
  Pallas kernels  45.7 us (97%)
  between operations  0.64 us (1%)
  local copies, waits for them, and re-layouts  0.58 us (1%)
    pallas_call x1, Pallas kernels, exchange(): pl.pallas_call(functools.partial(kernel, room), out_shape=(jax.ShapeDtype...  45.7 us

profile of v13, /device:TPU:1, one launch (start us, length us, event | category | flops | bytes accessed | tf_op | source)
XLA Modules:
  0.0 47.2 jit_solution(17844823535053812426)
XLA Ops:
  0.0 45.7 %shard_map.39 = (f32[4,128]{1,0:T(4,128)S(1)}, s32[1]{0:T(128)}) custom-call(bf16[512,768]{1,0:T(8,128)(2,1)} %emb_hbm.1, s32[4,128]{1,0:T(4,128)} %bitcast.2.cid_hbm, s32[4,128]{1,0:T(4,128)} %bitcast.3.rank_hbm), custom_call_target="tpu_custom_call" | custom-call | tf_op jit(solution)/shard_map/pallas_call | solution.py:445
  46.3 0.2 conditional.1
  46.6 0.6 %copy.10 = f32[512]{0:T(512)} copy(f32[512]{0:T(512)S(1)} %get-tuple-element.25) | data formatting | bytes 4096
